TPU v7x, 16 devices: a whole 2x2x2 slice. The times are simulated.
16 devices in a mesh: fsdp: 16 (over z, y, x, core).
Axes of the slice: x: 2, y: 2, z: 2, core: 2. Of those that a mesh axis runs over, the one named last changes fastest.
Arguments:
- grad_mat: bfloat16 [16, 21233664], P('fsdp')
- grad_vec: bfloat16 [16, 14336], P('fsdp')
- master_mat: float32 [21233664], P('fsdp')
- moment_mat: float32 [21233664], P('fsdp')
- second_mat: float32 [21233664], P('fsdp')
- master_vec: float32 [14336], P('fsdp')
- moment_vec: float32 [14336], P('fsdp')
- second_vec: float32 [14336], P('fsdp')
Outputs:
- output 1: float32 [21233664], P('fsdp')
- output 2: float32 [21233664], P('fsdp')
- output 3: float32 [21233664], P('fsdp')
- output 4: float32 [14336], P('fsdp')
- output 5: float32 [14336], P('fsdp')
- output 6: float32 [14336], P('fsdp')
- output 7: bfloat16 [21233664], replicated
- output 8: bfloat16 [14336], replicated
All inputs are finite; a program needn't handle non-finite values.
Results may differ from a plain program's by a relative error of at most 0.001.
Values are sent between devices in bfloat16 or wider.
A program may use at most 1 GiB of HBM per device.

v0:
```python
import jax
import jax.numpy as jnp
from jax import lax
from jax.sharding import PartitionSpec as P

STEP = 4
LEARN_RATE = 1e-3
BETA_ONE = 0.9
BETA_TWO = 0.999
ADAM_EPS = 1e-8
DECAY = 0.01
NORM_EPS = 1e-6
FIX_ONE = 1.0 - BETA_ONE ** STEP
FIX_TWO = 1.0 - BETA_TWO ** STEP


def adam_update(grad_sum, clip_coef, master, moment, second, decay):
    clip_grad = clip_coef * grad_sum
    new_moment = BETA_ONE * moment + (1.0 - BETA_ONE) * clip_grad
    new_second = BETA_TWO * second + (1.0 - BETA_TWO) * clip_grad * clip_grad
    step_dir = (new_moment / FIX_ONE) / (jnp.sqrt(new_second / FIX_TWO) + ADAM_EPS)
    new_master = master - LEARN_RATE * (step_dir + decay * master)
    return new_master, new_moment, new_second


def total_share(grad_block, group):
    rows = grad_block.reshape(group, grad_block.shape[1] // group)
    received = lax.all_to_all(rows, 'fsdp', 0, 0, tiled=True)
    return jnp.sum(received, axis=0, dtype=jnp.float32)


def solution(mesh):
    group = mesh.shape['fsdp']

    def local_step(grad_mat, grad_vec, master_mat, moment_mat, second_mat, master_vec, moment_vec, second_vec):
        sum_mat = total_share(grad_mat, group)
        sum_vec = total_share(grad_vec, group)
        local_square = jnp.sum(sum_mat * sum_mat) + jnp.sum(sum_vec * sum_vec)
        total_norm = jnp.sqrt(lax.psum(local_square, 'fsdp'))
        clip_coef = jnp.minimum(1.0, 1.0 / (total_norm + NORM_EPS))
        new_mat = adam_update(sum_mat, clip_coef, master_mat, moment_mat, second_mat, DECAY)
        new_vec = adam_update(sum_vec, clip_coef, master_vec, moment_vec, second_vec, 0.0)
        weights_mat = lax.all_gather(new_mat[0].astype(jnp.bfloat16), 'fsdp', tiled=True)
        weights_vec = lax.all_gather(new_vec[0].astype(jnp.bfloat16), 'fsdp', tiled=True)
        return new_mat + new_vec + (weights_mat, weights_vec)

    row_spec = P('fsdp', None)
    flat_spec = P('fsdp')
    whole_spec = P()
    return jax.shard_map(local_step, mesh=mesh,
                         in_specs=(row_spec, row_spec) + (flat_spec,) * 6,
                         out_specs=(flat_spec,) * 6 + (whole_spec, whole_spec),
                         check_vma=False)
```

profile of v0, /device:TPU:0, one launch (start us, length us, event | category | flops | bytes accessed | tf_op | source)
XLA Modules:
  0.0 1450.1 jit_solution(478940817215973270)
XLA Ops:
  7.2 0.5 broadcast.21
  7.7 1.6 reduce.4
  9.3 0.7 reshape.31
  10.0 5.3 all-to-all-start.1
  15.3 267.7 %reduce.3 = bf16[16,1327104]{1,0:T(8,128)(2,1)} reduce(bf16[16,1,1327104]{2,1,0:T(2,128)(2,1)} %bitcast, bf16[]{:T(256)} %broadcast.21), dimensions={1}, to_apply=%bitcast.reduce_sub_computation | reduce | bytes 84934656 | tf_op jit(solution)/shard_map/all_to_all | solution.py:28
  283.0 221.0 %reshape.29 = bf16[16,2,663552]{2,1,0:T(2,128)(2,1)} reshape(bf16[16,1327104]{1,0:T(8,128)(2,1)} %reduce.3) | data formatting | bytes 84934656
  504.0 5.0 all-to-all-start
  509.0 0.0 all-gather.3.cloned.1.call-start
  509.1 0.1 reshape.32
  509.2 0.1 convert_reduce_fusion.1
  509.3 0.6 multiply_reduce_fusion.1
  509.9 505.8 %all-to-all-done = bf16[16,2,663552]{2,1,0:T(2,128)(2,1)} async-done(((bf16[16,2,663552]{2,1,0:T(2,128)(2,1)}), bf16[16,2,663552]{2,1,0:T(2,128)(2,1)}, u32[]{:S(2)}, u32[]{:S(2)}) %all-to-all-start) | async-done | bytes 42467360 | tf_op jit(solution)/shard_map/all_to_all | solution.py:28
  1015.7 101.4 %reshape.30 = bf16[16,1,1327104]{2,1,0:T(2,128)(2,1)} reshape(bf16[16,2,663552]{2,1,0:T(2,128)(2,1)} %all-to-all-done) | data formatting | bytes 84934656
  1117.0 81.7 %convert_reduce_fusion = f32[1327104]{0:T(1024)S(1)} fusion(bf16[16,1,1327104]{2,1,0:T(2,128)(2,1)} %reshape.30), kind=kLoop, calls=%fused_computation | loop fusion | flops 41140224 | bytes 47775744 | tf_op jit(solution)/shard_map/reduce_sum | solution.py:29
  1198.8 2.4 copy-done
  1201.1 2.0 multiply_reduce_fusion
  1204.4 32.9 %psum.7 = f32[]{:T(128)} all-reduce(f32[]{:T(128)S(6)} %add.38), channel_id=1, replica_groups=mesh['fsdp'=16] {'fsdp'}, use_global_device_ids=true, to_apply=%region_4.0 | all-reduce | flops 1 | bytes 8 | tf_op jit(solution)/shard_map/psum | solution.py:39
  1238.0 15.0 %fusion.4 = (bf16[1327104]{0:T(1024)(128)(2,1)}, f32[1327104]{0:T(1024)}, f32[1327104]{0:T(1024)}, f32[1327104]{0:T(1024)}) fusion(f32[1327104]{0:T(1024)} %param.10, f32[1327104]{0:T(1024)} %copy-done, f32[]{:T(128)S(6)} %min.3, f32[1327104]{0:T(1024)} %param.11, f32[1327104]{0:T(1024)} %param.12), kind=kLoop, calls=%fused_computation.13 | loop fusion | flops 22560768 | bytes 39813124 | tf_op jit(solution)/shard_map/convert_element_type | solution.py:43
  1253.1 0.6 fusion.2
  1253.7 14.1 all-gather
  1267.8 0.2 reduce.2
  1267.9 0.7 reshape.27
  1268.6 146.1 %all-gather.3.cloned.1.call-done = bf16[21233664]{0:T(1024)(128)(2,1)} async-done(((bf16[1327104]{0:T(1024)(128)(2,1)}), bf16[21233664]{0:T(1024)(128)(2,1)}) %all-gather.3.cloned.1.call-update) | async-done | bytes 42467344 | tf_op jit(solution)/shard_map/all_gather | solution.py:43
  1414.7 28.5 %copy.17 = bf16[21233664]{0:T(1024)(128)(2,1)} copy(bf16[21233664]{0:T(1024)(128)(2,1)} %all-gather.3.cloned.1.call-done) | data formatting | bytes 84934656
  (10 shorter events, 0.0 us)
Async XLA Ops:
  10.0 494.0 %all-to-all-start.1 = ((bf16[16,2,448]{2,1,0:T(2,128)(2,1)}), bf16[16,2,448]{2,1,0:T(2,128)(2,1)S(1)}, u32[]{:S(2)}, u32[]{:S(2)}) async-start(bf16[16,2,448]{2,1,0:T(2,128)(2,1)} %reshape.31), calls=%async_computation.1 | async-start | bytes 65536 | tf_op jit(solution)/shard_map/all_to_all | solution.py:28
  504.0 511.7 %all-to-all-start = ((bf16[16,2,663552]{2,1,0:T(2,128)(2,1)}), bf16[16,2,663552]{2,1,0:T(2,128)(2,1)}, u32[]{:S(2)}, u32[]{:S(2)}) async-start(bf16[16,2,663552]{2,1,0:T(2,128)(2,1)} %reshape.29), calls=%async_computation | async-start | bytes 84934656 | tf_op jit(solution)/shard_map/all_to_all | solution.py:28
  509.0 905.6 %all-gather.3.cloned.1.call-start = ((), (), s32[]{:S(2)}) async-start(), calls=%async_computation.2 | async-start | bytes 45121536 | tf_op jit(solution)/shard_map/all_gather | solution.py:43
  1198.7 2.4 copy-start
  1238.0 15.1 %copy-start.1 = (f32[896]{0:T(1024)S(1)}, f32[896]{0:T(1024)}, u32[]{:S(2)}) copy-start(f32[896]{0:T(1024)} %param.13) | copy-start | bytes 10756
  1238.0 15.1 %copy-start.2 = (f32[896]{0:T(1024)S(1)}, f32[896]{0:T(1024)}, u32[]{:S(2)}) copy-start(f32[896]{0:T(1024)} %param.14) | copy-start | bytes 10756
  1238.0 15.1 %copy-start.3 = (f32[896]{0:T(1024)S(1)}, f32[896]{0:T(1024)}, u32[]{:S(2)}) copy-start(f32[896]{0:T(1024)} %param.15) | copy-start | bytes 10756
Sparse Core Ops, SparseCore 0:
  1253.2 161.4 all-gather.2
where the time goes:
time: 1460 us; the launch traced here: 1450 us
  waiting for transfers between devices  652 us (45%)
  other arithmetic  369 us (25%)
  local copies, waits for them, and re-layouts  355 us (24%)
  blocking collectives  46.9 us (3%)
  between operations  16.3 us (1%)
    all_to_all x2, waiting for transfers between devices, total_share(): received = lax.all_to_all(rows, 'fsdp', 0, 0, tiled=True)  506 us
    unnamed x15, local copies, waits for them, and re-layouts  355 us
    all_to_all x2, other arithmetic, total_share(): received = lax.all_to_all(rows, 'fsdp', 0, 0, tiled=True)  269 us
    all_gather x1, waiting for transfers between devices, local_step(): lax.all_gather(new_mat[0].astype(jnp.bfloat16), 'fsdp', tiled=True)  146 us
    reduce_sum x2, other arithmetic, total_share(): return jnp.sum(received, axis=0, dtype=jnp.float32)  81.8 us
    psum x1, blocking collectives, local_step(): total_norm = jnp.sqrt(lax.psum(local_square, 'fsdp'))  32.9 us
  transfers between devices with their start and end apart: 3, of which 2 were waited for; matrix products, arithmetic and copies ran while one was open for 34% of the time, Pallas kernels for 0%

commit v1 on v0

v1 whole, which is shorter than its diff:
```python
import functools

import jax
import jax.numpy as jnp
from jax import lax
from jax.experimental import pallas as pl
from jax.experimental.pallas import tpu as pltpu
from jax.sharding import PartitionSpec as P

STEP = 4
LEARN_RATE = 1e-3
BETA_ONE = 0.9
BETA_TWO = 0.999
ADAM_EPS = 1e-8
DECAY = 0.01
NORM_EPS = 1e-6
FIX_ONE = 1.0 - BETA_ONE ** STEP
FIX_TWO = 1.0 - BETA_TWO ** STEP

MESH = pl.DeviceIdType.MESH
LANES = 128
SLOTS = 3
STEPS = (2, 4, 8)
F32 = jnp.float32
BF16 = jnp.bfloat16


def adam_update(grad_sum, clip_coef, master, moment, second, decay):
    clip_grad = clip_coef * grad_sum
    new_moment = BETA_ONE * moment + (1.0 - BETA_ONE) * clip_grad
    new_second = BETA_TWO * second + (1.0 - BETA_TWO) * clip_grad * clip_grad
    step_dir = (new_moment / FIX_ONE) / (jnp.sqrt(new_second / FIX_TWO) + ADAM_EPS)
    new_master = master - LEARN_RATE * (step_dir + decay * master)
    return new_master, new_moment, new_second


def bit_of(index, stride):
    return lax.rem(lax.div(index, stride), 2)


def across(index, stride):
    return index + stride * (1 - 2 * bit_of(index, stride))


def reduce_kernel(chunks, rows, grad, gvec, total_out, vec_out, clip_out,
                  raw, packed, recv_a, send_b, keep_b, recv_b, send_c, keep_c, recv_c,
                  vec_in, square, square_in,
                  raw_sem, send_a_sem, recv_a_sem, send_b_sem, recv_b_sem, send_c_sem, recv_c_sem,
                  small_send, small_recv, free_sem):
    me = lax.axis_index('fsdp')
    core = bit_of(me, 1)
    group = 16

    barrier = pltpu.get_barrier_semaphore()
    for k in range(1, group):
        pl.semaphore_signal(barrier, inc=1, device_id=(lax.rem(me + k, group),), device_id_type=MESH)
    pl.semaphore_wait(barrier, group - 1)

    dims = [tuple(STEPS[(c + k) % 3] for k in range(3)) for c in range(3)]

    def load(c, t):
        slot = lax.rem(t + c, 2)
        return pltpu.make_async_copy(grad.at[:, c, t], raw.at[slot], raw_sem.at[slot])

    def peers(c):
        d1 = dims[c][0]
        other = across(me, d1)
        return ((across(me, 1), bit_of(me, d1), 1 - core),
                (other, 1 - bit_of(me, d1), core),
                (across(other, 1), 1 - bit_of(me, d1), 1 - core))

    def copy_a(c, t, j):
        device, d1_bit, core_bit = peers(c)[j]
        ps, rs = lax.rem(t, 2), lax.rem(t, SLOTS)
        return pltpu.make_async_remote_copy(
            src_ref=packed.at[c, ps, 2 * d1_bit + core_bit], dst_ref=recv_a.at[c, rs, j],
            send_sem=send_a_sem.at[c, ps, j], recv_sem=recv_a_sem.at[c, rs, j],
            device_id=(device,), device_id_type=MESH)

    def copy_b(c, t):
        s = lax.rem(t, 2)
        return pltpu.make_async_remote_copy(
            src_ref=send_b.at[c, s], dst_ref=recv_b.at[c, t],
            send_sem=send_b_sem.at[c, s], recv_sem=recv_b_sem.at[c, t],
            device_id=(across(me, dims[c][1]),), device_id_type=MESH)

    def copy_c(c, t):
        s = lax.rem(t, 2)
        return pltpu.make_async_remote_copy(
            src_ref=send_c.at[c, s], dst_ref=recv_c.at[c, t],
            send_sem=send_c_sem.at[c, s], recv_sem=recv_c_sem.at[c, t],
            device_id=(across(me, dims[c][2]),), device_id_type=MESH)

    blk = 96
    blocks = rows // blk

    def pack_and_send(c, t):
        load(c, t).wait()
        ps = lax.rem(t, 2)
        rs = lax.rem(t + c, 2)

        @pl.when(t >= 2)
        def _():
            for j in range(3):
                copy_a(c, t - 2, j).wait_send()

        d1, d2, d3 = dims[c]
        for share in range(group):
            bits = [(share // d) % 2 for d in (d1, 1, d2, d3)]
            quarter, part = 2 * bits[0] + bits[1], 2 * bits[2] + bits[3]

            def body(b, carry):
                start = pl.multiple_of(b * blk, blk)
                flat = raw[rs, share, :, pl.ds(pl.multiple_of(b * blk * LANES, blk * LANES), blk * LANES)]
                packed[c, ps, quarter, part, pl.ds(start, blk), :] = flat.reshape(blk, LANES)
                return carry

            lax.fori_loop(0, blocks, body, 0)

        @pl.when(t >= SLOTS)
        def _():
            for j in range(3):
                pl.semaphore_wait(free_sem.at[c, j], 1)

        for j in range(3):
            copy_a(c, t, j).start()

    def sum_a(c, t):
        ps, rs = lax.rem(t, 2), lax.rem(t, SLOTS)
        d1, d2, d3 = dims[c]
        mine = 2 * bit_of(me, d1) + core
        for j in range(3):
            copy_a(c, t, j).wait_recv()

        @pl.when(t >= 2)
        def _():
            copy_b(c, t - 2).wait_send()

        s = lax.rem(t, 2)
        for target, half in ((send_b, 1 - bit_of(me, d2)), (keep_b, bit_of(me, d2))):
            for k in range(2):
                part = 2 * half + k

                def body(b, carry):
                    here = pl.ds(pl.multiple_of(b * blk, blk), blk)
                    one = packed[c, ps, mine, part, here, :].astype(F32)
                    two = recv_a[c, rs, 0, part, here, :].astype(F32)
                    three = recv_a[c, rs, 1, part, here, :].astype(F32)
                    four = recv_a[c, rs, 2, part, here, :].astype(F32)
                    target[c, s, k, here, :] = (one + two) + (three + four)
                    return carry

                lax.fori_loop(0, blocks, body, 0)
            if target is send_b:
                copy_b(c, t).start()

        @pl.when(t + SLOTS < chunks)
        def _():
            for j in range(3):
                pl.semaphore_signal(free_sem.at[c, j], inc=1, device_id=(peers(c)[j][0],), device_id_type=MESH)

    def sum_b(c, t):
        d3 = dims[c][2]
        copy_b(c, t).wait_recv()

        @pl.when(t >= 2)
        def _():
            copy_c(c, t - 2).wait_send()

        s = lax.rem(t, 2)
        for target, k in ((send_c, 1 - bit_of(me, d3)), (keep_c, bit_of(me, d3))):
            def body(b, carry):
                here = pl.ds(pl.multiple_of(b * blk, blk), blk)
                target[c, s, here, :] = keep_b[c, s, k, here, :] + recv_b[c, t, k, here, :]
                return carry

            lax.fori_loop(0, blocks, body, 0)
            if target is send_c:
                copy_c(c, t).start()

    def sum_c(c, t):
        copy_c(c, t).wait_recv()
        s = lax.rem(t, 2)

        def body(b, running):
            here = pl.ds(pl.multiple_of(b * blk, blk), blk)
            there = pl.ds(pl.multiple_of((c * chunks + t) * rows + b * blk, blk), blk)
            total = keep_c[c, s, here, :] + recv_c[c, t, here, :]
            total_out[there, :] = total
            return running + jnp.sum((total * total).reshape(blk // 8, 8, LANES), axis=0)

        square[...] += lax.fori_loop(0, blocks, body, jnp.zeros((8, LANES), F32))

    def small_copy(src, dst, k, sem):
        return pltpu.make_async_remote_copy(
            src_ref=src, dst_ref=dst, send_sem=small_send.at[sem, k], recv_sem=small_recv.at[sem, k],
            device_id=(lax.rem(me + k, group),), device_id_type=MESH)

    def vec_copy(k):
        return small_copy(gvec.at[lax.rem(me + k, group)], vec_in.at[k], k, 0)

    def square_copy(k):
        return small_copy(square, square_in.at[k], k, 1)

    square[...] = jnp.zeros_like(square)
    for c in range(2):
        load(c, 0).start()
    for c in range(3):
        pack_and_send(c, 0)
        load((c + 2) % 3, (c + 2) // 3).start()
    for k in range(1, group):
        vec_copy(k).start()

    for c in range(3):
        pack_and_send(c, 1)
        load((c + 2) % 3, 1 + (c + 2) // 3).start()

    def tick(u, carry):
        for c in range(3):
            @pl.when(u < chunks)
            def _():
                sum_a(c, u)
        for c in range(3):
            @pl.when((u >= 1) & (u < chunks + 1))
            def _():
                sum_b(c, u - 1)
        for c in range(3):
            @pl.when(u >= 2)
            def _():
                sum_c(c, u - 2)
        for c in range(3):
            @pl.when(u + 2 < chunks)
            def _():
                pack_and_send(c, u + 2)

            nc, nt = (c + 2) % 3, u + 2 + (c + 2) // 3

            @pl.when(nt < chunks)
            def _():
                load(nc, nt).start()
        return carry

    lax.fori_loop(0, chunks + 2, tick, 0)

    vec_sum = gvec[me].astype(F32)
    for k in range(1, group):
        vec_copy(k).wait()
        vec_sum = vec_sum + vec_in[k].astype(F32)
    vec_out[...] = vec_sum
    square[0:1, :] += sum((vec_sum * vec_sum)[:, LANES * k:LANES * (k + 1)] for k in range(vec_sum.shape[1] // LANES))

    for k in range(1, group):
        square_copy(k).start()
    whole = square[...]
    for k in range(1, group):
        square_copy(k).wait_recv()
        whole = whole + square_in[k]
    for k in range(1, group):
        square_copy(k).wait_send()
    norm = jnp.sqrt(jnp.sum(whole, keepdims=True))
    clip_out[...] = jnp.broadcast_to(jnp.minimum(1.0, 1.0 / (norm + NORM_EPS)), clip_out.shape)

    for c in range(3):
        for t in range(chunks - 2, chunks):
            for j in range(3):
                copy_a(c, t, j).wait_send()
            copy_b(c, t).wait_send()
            copy_c(c, t).wait_send()


def reduce_share(grad_mat, grad_vec, group, chunks):
    share_rows = grad_mat.shape[1] // group // LANES
    rows = share_rows // (3 * chunks)
    vec_share = grad_vec.shape[1] // group
    grad = grad_mat.reshape(group, 3, chunks, 1, rows * LANES)
    gvec = grad_vec.reshape(group, 1, vec_share)
    vmem = pl.BlockSpec(memory_space=pltpu.VMEM)
    dma = pltpu.SemaphoreType.DMA
    total, vec, clip = pl.pallas_call(
        functools.partial(reduce_kernel, chunks, rows),
        out_shape=(jax.ShapeDtypeStruct((share_rows, LANES), F32),
                   jax.ShapeDtypeStruct((1, vec_share), F32),
                   jax.ShapeDtypeStruct((8, LANES), F32)),
        in_specs=[pl.BlockSpec(memory_space=pl.ANY), vmem],
        out_specs=(vmem, vmem, vmem),
        scratch_shapes=[
            pltpu.VMEM((2, group, 1, rows * LANES), BF16),
            pltpu.VMEM((3, 2, 4, 4, rows, LANES), BF16),
            pltpu.VMEM((3, SLOTS, 3, 4, rows, LANES), BF16),
            pltpu.VMEM((3, 2, 2, rows, LANES), F32),
            pltpu.VMEM((3, 2, 2, rows, LANES), F32),
            pltpu.VMEM((3, chunks, 2, rows, LANES), F32),
            pltpu.VMEM((3, 2, rows, LANES), F32),
            pltpu.VMEM((3, 2, rows, LANES), F32),
            pltpu.VMEM((3, chunks, rows, LANES), F32),
            pltpu.VMEM((group, 1, vec_share), BF16),
            pltpu.VMEM((8, LANES), F32),
            pltpu.VMEM((group, 8, LANES), F32),
            dma((2,)),
            dma((3, 2, 3)), dma((3, SLOTS, 3)),
            dma((3, 2)), dma((3, chunks)),
            dma((3, 2)), dma((3, chunks)),
            dma((2, group)), dma((2, group)),
            pltpu.SemaphoreType.REGULAR((3, 3)),
        ],
        compiler_params=pltpu.CompilerParams(collective_id=0, has_side_effects=True, vmem_limit_bytes=60 * 1024 * 1024),
        name='reduce_share',
    )(grad, gvec)
    return total.reshape(-1), vec.reshape(-1), clip[0, 0]


def solution(mesh):
    group = mesh.shape['fsdp']

    def local_step(grad_mat, grad_vec, master_mat, moment_mat, second_mat, master_vec, moment_vec, second_vec):
        sum_mat, sum_vec, clip_coef = reduce_share(grad_mat, grad_vec, group, 12)
        new_mat = adam_update(sum_mat, clip_coef, master_mat, moment_mat, second_mat, DECAY)
        new_vec = adam_update(sum_vec, clip_coef, master_vec, moment_vec, second_vec, 0.0)
        weights_mat = lax.all_gather(new_mat[0].astype(jnp.bfloat16), 'fsdp', tiled=True)
        weights_vec = lax.all_gather(new_vec[0].astype(jnp.bfloat16), 'fsdp', tiled=True)
        return new_mat + new_vec + (weights_mat, weights_vec)

    row_spec = P('fsdp', None)
    flat_spec = P('fsdp')
    whole_spec = P()
    return jax.shard_map(local_step, mesh=mesh,
                         in_specs=(row_spec, row_spec) + (flat_spec,) * 6,
                         out_specs=(flat_spec,) * 6 + (whole_spec, whole_spec),
                         check_vma=False)
```

time: 1460 us -> 509 us (0.35)
  waiting for transfers between devices: 652 us -> 146 us
  other arithmetic: 369 us -> 17.1 us
  local copies, waits for them, and re-layouts: 355 us -> 30.3 us
  Pallas kernels: 0 us -> 288 us
  blocking collectives: 46.9 us -> 13.1 us
    all_to_all x2 -> x0, waiting for transfers between devices: 506 us -> none  [total_share(): received = lax.all_to_all(rows, 'fsdp', 0, 0, tiled=True)]
    unnamed x15 -> x11, local copies, waits for them, and re-layouts: 355 us -> 29.1 us
    pallas_call x0 -> x1, Pallas kernels: none -> 288 us  [reduce_share(): pl.pallas_call(functools.partial(reduce_kernel, chunks, rows), out_shape=...]
    all_to_all x2 -> x0, other arithmetic: 269 us -> none  [total_share(): received = lax.all_to_all(rows, 'fsdp', 0, 0, tiled=True)]
    reduce_sum x4 -> x0, other arithmetic: 84.3 us -> none  [the longest x2 81.8 us: total_share(): return jnp.sum(received, axis=0, dtype=jnp.float32)]
    psum x1 -> x0, blocking collectives: 32.9 us -> none  [local_step(): total_norm = jnp.sqrt(lax.psum(local_square, 'fsdp'))]
  transfers between devices with their start and end apart: 3 -> 1, of which waited for: 2 -> 1; matrix products, arithmetic and copies ran while one was open for 34% -> 0% of each run, Pallas kernels for 0% -> 0%
where the time goes in v1:
time: 509 us; the launch traced here: 508 us
  Pallas kernels  288 us (57%)
  waiting for transfers between devices  146 us (29%)
  local copies, waits for them, and re-layouts  30.3 us (6%)
  other arithmetic  17.1 us (3%)
  between operations  14.1 us (3%)
  blocking collectives  13.1 us (3%)
    pallas_call x1, Pallas kernels, reduce_share(): pl.pallas_call(functools.partial(reduce_kernel, chunks, rows), out_shape=...  288 us
    all_gather x1, waiting for transfers between devices, local_step(): lax.all_gather(new_mat[0].astype(jnp.bfloat16), 'fsdp', tiled=True)  145 us
    unnamed x11, local copies, waits for them, and re-layouts  29.1 us
    convert_element_type x1, other arithmetic, local_step(): new_mat[0].astype(jnp.bfloat16)  15.7 us
    all_gather x1, blocking collectives, local_step(): lax.all_gather(new_vec[0].astype(jnp.bfloat16), 'fsdp', tiled=True)  13.1 us
  transfers between devices with their start and end apart: 1, of which 1 were waited for; matrix products, arithmetic and copies ran while one was open for 0% of the time, Pallas kernels for 0%

profile of v1, /device:TPU:0, one launch (start us, length us, event | category | flops | bytes accessed | tf_op | source)
XLA Modules:
  0.0 508.1 jit_solution(4792423909263711613)
XLA Ops:
  7.2 0.0 all-gather.3.cloned.1.call-start
  7.2 287.9 %reduce_share.1 = (f32[10368,128]{1,0:T(8,128)}, f32[1,896]{1,0:T(1,128)}, f32[8,128]{1,0:T(8,128)}) custom-call(bf16[16,3,12,1,36864]{4,3,2,1,0:T(2,128)(2,1)} %bitcast.grad, bf16[16,1,896]{2,1,0:T(2,128)(2,1)} %bitcast.10), custom_call_target="tpu_custom_call" | custom-call | tf_op jit(solution)/shard_map/reduce_share/pallas_call | solution.py:279
  295.1 1.2 slice.3
  296.3 0.0 copy-start.3
  296.3 0.0 copy-start
  296.3 0.0 copy-start.1
  296.3 0.0 copy-start.2
  296.3 15.7 %fusion.5 = (bf16[1327104]{0:T(1024)(128)(2,1)}, f32[1327104]{0:T(1024)}, f32[1327104]{0:T(1024)}, f32[1327104]{0:T(1024)}) fusion(f32[1327104]{0:T(1024)} %param.10, f32[10368,128]{1,0:T(8,128)} %get-tuple-element.12, f32[]{:T(128)} %bitcast.2, f32[1327104]{0:T(1024)} %param.11, f32[1327104]{0:T(1024)} %param.12), kind=kLoop, calls=%fused_computation.11 | loop fusion | flops 22560768 | bytes 39813124 | tf_op jit(solution)/shard_map/convert_element_type | solution.py:319
  312.0 0.0 all-gather.3.cloned.1.call-update
  312.0 0.0 copy-done.3
  312.0 0.7 multiply_reduce_fusion
  312.7 0.0 copy-done
  312.7 0.0 copy-done.1
  312.7 0.0 copy-done.2
  312.7 0.6 fusion.3
  313.4 13.1 %all-gather = bf16[16,1,896]{2,1,0:T(2,128)(2,1)S(1)} all-gather(bf16[1,1,896]{2,1,0:T(2,128)(2,1)S(1)} %reshape.30), channel_id=1, replica_groups=mesh['fsdp'=16] {'fsdp'}, dimensions={0}, use_global_device_ids=true | all-gather | bytes 30464 | tf_op jit(solution)/shard_map/all_gather | solution.py:320
  326.5 0.2 reduce.1
  326.7 0.7 reshape.31
  327.3 145.5 %all-gather.3.cloned.1.call-done = bf16[21233664]{0:T(1024)(128)(2,1)} async-done(((bf16[1327104]{0:T(1024)(128)(2,1)}), bf16[21233664]{0:T(1024)(128)(2,1)}) %all-gather.3.cloned.1.call-update) | async-done | bytes 42467344 | tf_op jit(solution)/shard_map/all_gather | solution.py:319
  472.8 28.5 %copy.17 = bf16[21233664]{0:T(1024)(128)(2,1)} copy(bf16[21233664]{0:T(1024)(128)(2,1)} %all-gather.3.cloned.1.call-done) | data formatting | bytes 84934656
  (1 shorter events, 0.0 us)
Async XLA Ops:
  7.2 465.7 %all-gather.3.cloned.1.call-start = ((), (), s32[]{:S(2)}) async-start(), calls=%async_computation | async-start | bytes 45121536 | tf_op jit(solution)/shard_map/all_gather | solution.py:319
  296.3 15.7 %copy-start.3 = (f32[1,896]{1,0:T(1,128)S(1)}, f32[1,896]{1,0:T(1,128)}, u32[]{:S(2)}) copy-start(f32[1,896]{1,0:T(1,128)} %get-tuple-element.13) | copy-start | bytes 10756
  296.3 16.4 %copy-start = (f32[896]{0:T(1024)S(1)}, f32[896]{0:T(1024)}, u32[]{:S(2)}) copy-start(f32[896]{0:T(1024)} %param.13) | copy-start | bytes 10756
  296.3 16.4 %copy-start.1 = (f32[896]{0:T(1024)S(1)}, f32[896]{0:T(1024)}, u32[]{:S(2)}) copy-start(f32[896]{0:T(1024)} %param.14) | copy-start | bytes 10756
  296.3 16.4 %copy-start.2 = (f32[896]{0:T(1024)S(1)}, f32[896]{0:T(1024)}, u32[]{:S(2)}) copy-start(f32[896]{0:T(1024)} %param.15) | copy-start | bytes 10756
Sparse Core Ops, SparseCore 0:
  312.1 160.6 all-gather.2

commit v2 on v1

--- a/solution.py
+++ b/solution.py
@@ -309,6 +309,126 @@
     return total.reshape(-1), vec.reshape(-1), clip[0, 0]
 
 
+def gather_kernel(chunks, rows, share, vec, out, vec_out, send_sem, recv_sem, vec_send, vec_recv, vec_local):
+    me = lax.axis_index('fsdp')
+    group = 16
+
+    barrier = pltpu.get_barrier_semaphore()
+    for k in range(1, group):
+        pl.semaphore_signal(barrier, inc=1, device_id=(lax.rem(me + k, group),), device_id_type=MESH)
+    pl.semaphore_wait(barrier, group - 1)
+
+    def flip(index, strides):
+        for stride in strides:
+            index = across(index, stride)
+        return index
+
+    def message(c, k, origin, step, sem):
+        source = flip(me, origin)
+        src = share.at[c, k] if not origin else out.at[source, c, k]
+        mask = sum(origin) + step
+        return pltpu.make_async_remote_copy(
+            src_ref=src, dst_ref=out.at[source, c, k],
+            send_sem=send_sem, recv_sem=recv_sem.at[c, k, mask],
+            device_id=(across(me, step),), device_id_type=MESH)
+
+    def arrived(c, k, origin):
+        pltpu.make_async_remote_copy(
+            src_ref=out.at[me, c, k], dst_ref=out.at[flip(me, origin), c, k],
+            send_sem=send_sem, recv_sem=recv_sem.at[c, k, sum(origin)],
+            device_id=(across(me, 1),), device_id_type=MESH).wait_recv()
+
+    def forward(c, k, origin, steps):
+        if origin:
+            arrived(c, k, origin)
+        for step in steps:
+            message(c, k, origin, step, send_sem).start()
+
+    dims = [tuple(STEPS[(c + j) % 3] for j in range(3)) for c in range(3)]
+
+    def vec_copy(k):
+        return pltpu.make_async_remote_copy(
+            src_ref=vec, dst_ref=vec_out.at[me], send_sem=vec_send.at[k], recv_sem=vec_recv.at[k],
+            device_id=(lax.rem(me + k, group),), device_id_type=MESH)
+
+    for which in range(3):
+        for c in range(3):
+            for k in range(chunks):
+                forward(c, k, (), (dims[c][which],))
+    for c in range(3):
+        for k in range(chunks):
+            forward(c, k, (), (1,))
+    for k in range(1, group):
+        vec_copy(k).start()
+    out[me] = share[...]
+    vec_out[me] = vec[...]
+    for c in range(3):
+        d1, d2, d3 = dims[c]
+        for k in range(chunks):
+            forward(c, k, (d1,), (d2, d3, 1))
+    for c in range(3):
+        d1, d2, d3 = dims[c]
+        for k in range(chunks):
+            forward(c, k, (d2,), (d3, 1))
+    for c in range(3):
+        d1, d2, d3 = dims[c]
+        for k in range(chunks):
+            forward(c, k, (d3,), (1,))
+    for c in range(3):
+        d1, d2, d3 = dims[c]
+        for k in range(chunks):
+            forward(c, k, (d1, d2), (d3, 1))
+    for origin in ((0, 2), (1, 2), (0, 1, 2)):
+        for c in range(3):
+            for k in range(chunks):
+                forward(c, k, tuple(dims[c][j] for j in origin), (1,))
+    for mask in range(8):
+        for c in range(3):
+            for k in range(chunks):
+                arrived(c, k, tuple(STEPS[j] for j in range(3) if mask // 2 ** j % 2) + (1,))
+    for k in range(1, group):
+        pltpu.make_async_remote_copy(
+            src_ref=vec, dst_ref=vec_out.at[lax.rem(me + group - k, group)], send_sem=vec_send.at[k],
+            recv_sem=vec_recv.at[k], device_id=(lax.rem(me + k, group),), device_id_type=MESH).wait()
+    pltpu.make_async_copy(out.at[pl.ds(0, group - 1)], out.at[pl.ds(0, group - 1)], send_sem).wait()
+
+
+def drain_kernel(parts, held, out, sem):
+    size = held.shape[0] // parts
+    copies = [pltpu.make_async_copy(held.at[pl.ds(k * size, size)], out.at[pl.ds(k * size, size)], sem.at[k])
+              for k in range(parts)]
+    for copy in copies:
+        copy.start()
+    for copy in copies:
+        copy.wait()
+
+
+def gather_share(share, vec, group, chunks):
+    rows = share.shape[0] // LANES // (3 * chunks)
+    vmem = pl.BlockSpec(memory_space=pltpu.VMEM)
+    dma = pltpu.SemaphoreType.DMA
+    weights, vec_weights = pl.pallas_call(
+        functools.partial(gather_kernel, chunks, rows),
+        out_shape=(pltpu.VMEM((group, 3, chunks, rows, LANES), BF16),
+                   jax.ShapeDtypeStruct((group, 1, vec.shape[0]), BF16)),
+        in_specs=[vmem, vmem],
+        out_specs=(vmem, vmem),
+        scratch_shapes=[dma, dma((3, chunks, 16)), dma((group,)), dma((group,)), dma],
+        compiler_params=pltpu.CompilerParams(collective_id=1, has_side_effects=True, vmem_limit_bytes=8 * 1024 * 1024),
+        name='gather_share',
+    )(share.reshape(3, chunks, rows, LANES), vec.reshape(1, -1))
+    weights = pl.pallas_call(
+        functools.partial(drain_kernel, 8),
+        out_shape=jax.ShapeDtypeStruct(weights.shape, BF16),
+        in_specs=[vmem],
+        out_specs=pl.BlockSpec(memory_space=pl.ANY),
+        scratch_shapes=[dma((8,))],
+        compiler_params=pltpu.CompilerParams(vmem_limit_bytes=8 * 1024 * 1024),
+        name='drain',
+    )(weights)
+    return weights.reshape(-1), vec_weights.reshape(-1)
+
+
 def solution(mesh):
     group = mesh.shape['fsdp']
 
@@ -316,8 +436,7 @@
         sum_mat, sum_vec, clip_coef = reduce_share(grad_mat, grad_vec, group, 12)
         new_mat = adam_update(sum_mat, clip_coef, master_mat, moment_mat, second_mat, DECAY)
         new_vec = adam_update(sum_vec, clip_coef, master_vec, moment_vec, second_vec, 0.0)
-        weights_mat = lax.all_gather(new_mat[0].astype(jnp.bfloat16), 'fsdp', tiled=True)
-        weights_vec = lax.all_gather(new_vec[0].astype(jnp.bfloat16), 'fsdp', tiled=True)
+        weights_mat, weights_vec = gather_share(new_mat[0].astype(BF16), new_vec[0].astype(BF16), group, 2)
         return new_mat + new_vec + (weights_mat, weights_vec)
 
     row_spec = P('fsdp', None)

time: 509 us -> 466 us (0.916)
  Pallas kernels: 288 us -> 445 us
  waiting for transfers between devices: 146 us -> 0 us
  local copies, waits for them, and re-layouts: 30.3 us -> 1.86 us
  between operations: 14.1 us -> 0.72 us
  blocking collectives: 13.1 us -> 0 us
    pallas_call x0 -> x2, Pallas kernels: none -> 157 us  [the longest x1 143 us: gather_share(): pl.pallas_call(functools.partial(gather_kernel, chunks, rows), out_shape=...]
    all_gather x1 -> x0, waiting for transfers between devices: 145 us -> none  [local_step(): lax.all_gather(new_mat[0].astype(jnp.bfloat16), 'fsdp', tiled=True)]
    unnamed x11 -> x6, local copies, waits for them, and re-layouts: 29.1 us -> 0.01 us
    all_gather x1 -> x0, blocking collectives: 13.1 us -> none  [local_step(): lax.all_gather(new_vec[0].astype(jnp.bfloat16), 'fsdp', tiled=True)]
  transfers between devices with their start and end apart: 1 -> 0, of which waited for: 1 -> 0; matrix products, arithmetic and copies ran while one was open for 0% -> 0% of each run, Pallas kernels for 0% -> 0%
where the time goes in v2:
time: 466 us; the launch traced here: 465 us
  Pallas kernels  445 us (95%)
  other arithmetic  17.3 us (4%)
    pallas_call x1, Pallas kernels, reduce_share(): pl.pallas_call(functools.partial(reduce_kernel, chunks, rows), out_shape=...  288 us
    pallas_call x1, Pallas kernels, gather_share(): pl.pallas_call(functools.partial(gather_kernel, chunks, rows), out_shape=...  143 us
    convert_element_type x1, other arithmetic, local_step(): new_mat[0].astype(BF16)  15.2 us
    pallas_call x1, Pallas kernels, gather_share(): pl.pallas_call(functools.partial(drain_kernel, 8), out_shape=jax.ShapeDty...  13.8 us

profile of v2, /device:TPU:0, one launch (start us, length us, event | category | flops | bytes accessed | tf_op | source)
XLA Modules:
  0.0 464.9 jit_solution(10471109348479010065)
XLA Ops:
  0.6 0.0 copy-start
  0.6 0.0 copy-start.1
  0.7 0.0 copy-start.2
  0.7 287.9 %reduce_share.1 = (f32[10368,128]{1,0:T(8,128)}, f32[1,896]{1,0:T(1,128)}, f32[8,128]{1,0:T(8,128)}) custom-call(bf16[16,3,12,1,36864]{4,3,2,1,0:T(2,128)(2,1)} %bitcast.grad, bf16[16,1,896]{2,1,0:T(2,128)(2,1)} %bitcast.14), custom_call_target="tpu_custom_call" | custom-call | tf_op jit(solution)/shard_map/reduce_share/pallas_call | solution.py:279
  288.6 1.2 slice.3
  289.7 1.3 multiply_reduce_fusion
  291.1 0.0 copy-done
  291.1 0.0 copy-done.1
  291.1 0.0 copy-done.2
  291.1 0.6 fusion.3
  291.7 15.2 %fusion.5 = (bf16[1327104]{0:T(1024)(128)(2,1)S(1)}, f32[1327104]{0:T(1024)}, f32[1327104]{0:T(1024)}, f32[1327104]{0:T(1024)}) fusion(f32[1327104]{0:T(1024)} %param.10, f32[10368,128]{1,0:T(8,128)} %get-tuple-element.14, f32[]{:T(128)} %bitcast.2, f32[1327104]{0:T(1024)} %param.11, f32[1327104]{0:T(1024)} %param.12), kind=kLoop, calls=%fused_computation.11 | loop fusion | flops 22560768 | bytes 39813124 | tf_op jit(solution)/shard_map/convert_element_type | solution.py:439
  307.0 143.3 %gather_share.1 = (bf16[16,3,2,1728,128]{4,3,2,1,0:T(8,128)(2,1)S(1)}, bf16[16,1,896]{2,1,0:T(2,128)(2,1)S(1)}) custom-call(bf16[3,2,1728,128]{3,2,1,0:T(8,128)(2,1)S(1)} %bitcast.12, bf16[1,896]{1,0:T(2,128)(2,1)S(1)} %reshape.43.vec), custom_call_target="tpu_custom_call" | custom-call | tf_op jit(solution)/shard_map/gather_share/pallas_call | solution.py:410
  450.3 13.8 %drain.1 = bf16[16,3,2,1728,128]{4,3,2,1,0:T(8,128)(2,1)} custom-call(bf16[16,3,2,1728,128]{4,3,2,1,0:T(8,128)(2,1)S(1)} %get-tuple-element.16.held), custom_call_target="tpu_custom_call" | custom-call | tf_op jit(solution)/shard_map/drain/pallas_call | solution.py:420
  464.0 0.2 reduce.1
  464.2 0.7 reshape.45
  (1 shorter events, 0.0 us)
Async XLA Ops:
  0.6 290.5 %copy-start = (f32[896]{0:T(1024)S(1)}, f32[896]{0:T(1024)}, u32[]{:S(2)}) copy-start(f32[896]{0:T(1024)} %param.13) | copy-start | bytes 10756
  0.6 290.5 %copy-start.1 = (f32[896]{0:T(1024)S(1)}, f32[896]{0:T(1024)}, u32[]{:S(2)}) copy-start(f32[896]{0:T(1024)} %param.14) | copy-start | bytes 10756
  0.7 290.5 %copy-start.2 = (f32[896]{0:T(1024)S(1)}, f32[896]{0:T(1024)}, u32[]{:S(2)}) copy-start(f32[896]{0:T(1024)} %param.15) | copy-start | bytes 10756

commit v3 on v2

--- a/solution.py
+++ b/solution.py
@@ -306,30 +306,43 @@
         compiler_params=pltpu.CompilerParams(collective_id=0, has_side_effects=True, vmem_limit_bytes=60 * 1024 * 1024),
         name='reduce_share',
     )(grad, gvec)
-    return total.reshape(-1), vec.reshape(-1), clip[0, 0]
-
-
-def gather_kernel(chunks, rows, share, vec, out, vec_out, send_sem, recv_sem, vec_send, vec_recv, vec_local):
+    return total, vec, clip
+
+
+def gather_kernel(chunks, rows, grad, clip, master, moment, second, vec_grad, vec_master, vec_moment, vec_second,
+                  out, new_master, new_moment, new_second, vec_out, new_vec_master, new_vec_moment, new_vec_second,
+                  grad_buf, vec_share, send_sem, recv_sem, load_sem, vec_send, vec_recv):
     me = lax.axis_index('fsdp')
     group = 16
 
+    def state_loads(c, k):
+        return [pltpu.make_async_copy(src.at[c, k], dst.at[c, k], load_sem.at[c, k, j])
+                for j, (src, dst) in enumerate(((master, new_master), (moment, new_moment), (second, new_second)))]
+
+    def grad_load(c, k):
+        return pltpu.make_async_copy(grad.at[c, k], grad_buf.at[(k * 3 + c) % 2], load_sem.at[c, k, 3])
+
+    order = [(c, k) for k in range(chunks) for c in range(3)]
+    for n, (c, k) in enumerate(order):
+        if n < 2:
+            grad_load(c, k).start()
+        for load in state_loads(c, k):
+            load.start()
+
     barrier = pltpu.get_barrier_semaphore()
     for k in range(1, group):
         pl.semaphore_signal(barrier, inc=1, device_id=(lax.rem(me + k, group),), device_id_type=MESH)
-    pl.semaphore_wait(barrier, group - 1)
 
     def flip(index, strides):
         for stride in strides:
             index = across(index, stride)
         return index
 
-    def message(c, k, origin, step, sem):
+    def message(c, k, origin, step):
         source = flip(me, origin)
-        src = share.at[c, k] if not origin else out.at[source, c, k]
-        mask = sum(origin) + step
-        return pltpu.make_async_remote_copy(
-            src_ref=src, dst_ref=out.at[source, c, k],
-            send_sem=send_sem, recv_sem=recv_sem.at[c, k, mask],
+        return pltpu.make_async_remote_copy(
+            src_ref=out.at[source, c, k], dst_ref=out.at[source, c, k],
+            send_sem=send_sem, recv_sem=recv_sem.at[c, k, sum(origin) + step],
             device_id=(across(me, step),), device_id_type=MESH)
 
     def arrived(c, k, origin):
@@ -339,29 +352,55 @@
             device_id=(across(me, 1),), device_id_type=MESH).wait_recv()
 
     def forward(c, k, origin, steps):
-        if origin:
-            arrived(c, k, origin)
+        arrived(c, k, origin)
         for step in steps:
-            message(c, k, origin, step, send_sem).start()
+            message(c, k, origin, step).start()
 
     dims = [tuple(STEPS[(c + j) % 3] for j in range(3)) for c in range(3)]
+    clip_coef = clip[0:1, :]
+    blk = 48
+
+    def update(c, k, slot):
+        def body(b, carry):
+            here = pl.ds(pl.multiple_of(b * blk, blk), blk)
+            p, m, v = adam_update(grad_buf[slot, here, :], clip_coef, new_master[c, k, here, :],
+                                  new_moment[c, k, here, :], new_second[c, k, here, :], DECAY)
+            new_master[c, k, here, :] = p
+            new_moment[c, k, here, :] = m
+            new_second[c, k, here, :] = v
+            out[me, c, k, here, :] = p.astype(BF16)
+            return carry
+
+        lax.fori_loop(0, rows // blk, body, 0)
+
+    for n, (c, k) in enumerate(order):
+        grad_load(c, k).wait()
+        for load in state_loads(c, k):
+            load.wait()
+        update(c, k, n % 2)
+        if n + 2 < len(order):
+            grad_load(*order[n + 2]).start()
+        if n == 0:
+            pl.semaphore_wait(barrier, group - 1)
+        for step in dims[c] + (1,):
+            message(c, k, (), step).start()
 
     def vec_copy(k):
         return pltpu.make_async_remote_copy(
-            src_ref=vec, dst_ref=vec_out.at[me], send_sem=vec_send.at[k], recv_sem=vec_recv.at[k],
+            src_ref=vec_share, dst_ref=vec_out.at[me], send_sem=vec_send.at[k], recv_sem=vec_recv.at[k],
             device_id=(lax.rem(me + k, group),), device_id_type=MESH)
 
-    for which in range(3):
-        for c in range(3):
-            for k in range(chunks):
-                forward(c, k, (), (dims[c][which],))
-    for c in range(3):
-        for k in range(chunks):
-            forward(c, k, (), (1,))
+    width = vec_share.shape[1]
+    p, m, v = adam_update(vec_grad[...], clip[0:1, 0:1], vec_master[...].reshape(1, width), vec_moment[...].reshape(1, width),
+                          vec_second[...].reshape(1, width), 0.0)
+    new_vec_master[...] = p
+    new_vec_moment[...] = m
+    new_vec_second[...] = v
+    vec_share[...] = p.astype(BF16)
+    vec_out[me] = p.astype(BF16)
     for k in range(1, group):
         vec_copy(k).start()
-    out[me] = share[...]
-    vec_out[me] = vec[...]
+
     for c in range(3):
         d1, d2, d3 = dims[c]
         for k in range(chunks):
@@ -388,56 +427,67 @@
                 arrived(c, k, tuple(STEPS[j] for j in range(3) if mask // 2 ** j % 2) + (1,))
     for k in range(1, group):
         pltpu.make_async_remote_copy(
-            src_ref=vec, dst_ref=vec_out.at[lax.rem(me + group - k, group)], send_sem=vec_send.at[k],
+            src_ref=vec_share, dst_ref=vec_out.at[lax.rem(me + group - k, group)], send_sem=vec_send.at[k],
             recv_sem=vec_recv.at[k], device_id=(lax.rem(me + k, group),), device_id_type=MESH).wait()
     pltpu.make_async_copy(out.at[pl.ds(0, group - 1)], out.at[pl.ds(0, group - 1)], send_sem).wait()
 
 
-def drain_kernel(parts, held, out, sem):
-    size = held.shape[0] // parts
-    copies = [pltpu.make_async_copy(held.at[pl.ds(k * size, size)], out.at[pl.ds(k * size, size)], sem.at[k])
-              for k in range(parts)]
+def drain_kernel(parts, *refs):
+    held, out, sem = refs[:4], refs[5:9], refs[-1]
+    copies = []
+    for j in range(4):
+        pieces = parts if j == 0 else 1
+        size = held[j].shape[0] // pieces
+        copies += [pltpu.make_async_copy(held[j].at[pl.ds(k * size, size)], out[j].at[pl.ds(k * size, size)],
+                                         sem.at[len(copies) + k]) for k in range(pieces)]
     for copy in copies:
         copy.start()
+    vec, vec_out = refs[4], refs[9]
+    vec_out[...] = jnp.concatenate([vec[k].astype(F32).reshape(-1, LANES) for k in range(vec.shape[0])], axis=0).astype(BF16)
     for copy in copies:
         copy.wait()
 
 
-def gather_share(share, vec, group, chunks):
-    rows = share.shape[0] // LANES // (3 * chunks)
-    vmem = pl.BlockSpec(memory_space=pltpu.VMEM)
+def update_and_gather(total, clip, state, vec_grad, vec_state, group, chunks):
+    rows = total.shape[0] // (3 * chunks)
+    width = vec_grad.shape[1]
+    shape = (3, chunks, rows, LANES)
+    vmem, anywhere = pl.BlockSpec(memory_space=pltpu.VMEM), pl.BlockSpec(memory_space=pl.ANY)
     dma = pltpu.SemaphoreType.DMA
-    weights, vec_weights = pl.pallas_call(
+    vec_shape = jax.ShapeDtypeStruct((1, width), F32)
+    results = pl.pallas_call(
         functools.partial(gather_kernel, chunks, rows),
-        out_shape=(pltpu.VMEM((group, 3, chunks, rows, LANES), BF16),
-                   jax.ShapeDtypeStruct((group, 1, vec.shape[0]), BF16)),
-        in_specs=[vmem, vmem],
-        out_specs=(vmem, vmem),
-        scratch_shapes=[dma, dma((3, chunks, 16)), dma((group,)), dma((group,)), dma],
-        compiler_params=pltpu.CompilerParams(collective_id=1, has_side_effects=True, vmem_limit_bytes=8 * 1024 * 1024),
-        name='gather_share',
-    )(share.reshape(3, chunks, rows, LANES), vec.reshape(1, -1))
-    weights = pl.pallas_call(
-        functools.partial(drain_kernel, 8),
-        out_shape=jax.ShapeDtypeStruct(weights.shape, BF16),
-        in_specs=[vmem],
-        out_specs=pl.BlockSpec(memory_space=pl.ANY),
-        scratch_shapes=[dma((8,))],
-        compiler_params=pltpu.CompilerParams(vmem_limit_bytes=8 * 1024 * 1024),
+        out_shape=(pltpu.VMEM((group,) + shape, BF16),) + (pltpu.VMEM(shape, F32),) * 3
+        + (jax.ShapeDtypeStruct((group, 1, width), BF16),) + (vec_shape,) * 3,
+        in_specs=[anywhere, vmem] + [anywhere] * 3 + [vmem] * 4,
+        out_specs=(vmem,) * 8,
+        scratch_shapes=[pltpu.VMEM((2, rows, LANES), F32), pltpu.VMEM((1, width), BF16),
+                        dma, dma((3, chunks, 16)), dma((3, chunks, 4)), dma((group,)), dma((group,))],
+        compiler_params=pltpu.CompilerParams(collective_id=1, has_side_effects=True, vmem_limit_bytes=4 * 1024 * 1024),
+        name='update_gather',
+    )(total.reshape(shape), clip, *[x.reshape(shape) for x in state], vec_grad, *vec_state)
+    parts = 8
+    drained = pl.pallas_call(
+        functools.partial(drain_kernel, parts),
+        out_shape=tuple(jax.ShapeDtypeStruct(x.shape, x.dtype) for x in results[:4])
+        + (jax.ShapeDtypeStruct((group * width // LANES, LANES), BF16),),
+        in_specs=[vmem] * 5,
+        out_specs=(anywhere,) * 4 + (vmem,),
+        scratch_shapes=[dma((parts + 3,))],
+        compiler_params=pltpu.CompilerParams(vmem_limit_bytes=4 * 1024 * 1024),
         name='drain',
-    )(weights)
-    return weights.reshape(-1), vec_weights.reshape(-1)
+    )(*[pltpu.with_memory_space_constraint(x, pltpu.VMEM) for x in results[:4]], results[4])
+    flat = [x.reshape(-1) for x in drained]
+    return tuple(flat[1:4]) + tuple(x.reshape(-1) for x in results[5:8]) + (flat[0], flat[4])
 
 
 def solution(mesh):
     group = mesh.shape['fsdp']
 
     def local_step(grad_mat, grad_vec, master_mat, moment_mat, second_mat, master_vec, moment_vec, second_vec):
-        sum_mat, sum_vec, clip_coef = reduce_share(grad_mat, grad_vec, group, 12)
-        new_mat = adam_update(sum_mat, clip_coef, master_mat, moment_mat, second_mat, DECAY)
-        new_vec = adam_update(sum_vec, clip_coef, master_vec, moment_vec, second_vec, 0.0)
-        weights_mat, weights_vec = gather_share(new_mat[0].astype(BF16), new_vec[0].astype(BF16), group, 2)
-        return new_mat + new_vec + (weights_mat, weights_vec)
+        total, vec_grad, clip = reduce_share(grad_mat, grad_vec, group, 12)
+        return update_and_gather(total, clip, (master_mat, moment_mat, second_mat), vec_grad,
+                                 (master_vec, moment_vec, second_vec), group, 4)
 
     row_spec = P('fsdp', None)
     flat_spec = P('fsdp')

time: 466 us -> 457 us (0.981)
  other arithmetic: 17.3 us -> 1.82 us
  Pallas kernels: 445 us -> 454 us
    convert_element_type x2 -> x0, other arithmetic: 15.8 us -> none  [the longest x1 15.2 us: local_step(): new_mat[0].astype(BF16)]
    pallas_call x2, Pallas kernels: 157 us -> 166 us  [the longest x1 146 us: update_and_gather(): pl.pallas_call(functools.partial(gather_kernel, chunks, rows), out_shape=...]
where the time goes in v3:
time: 457 us; the launch traced here: 456 us
  Pallas kernels  454 us (99%)
    pallas_call x1, Pallas kernels, reduce_share(): pl.pallas_call(functools.partial(reduce_kernel, chunks, rows), out_shape=...  288 us
    pallas_call x1, Pallas kernels, update_and_gather(): pl.pallas_call(functools.partial(gather_kernel, chunks, rows), out_shape=...  146 us
    pallas_call x1, Pallas kernels, update_and_gather(): pl.pallas_call(functools.partial(drain_kernel, parts), out_shape=tuple((j...  20 us

profile of v3, /device:TPU:0, one launch (start us, length us, event | category | flops | bytes accessed | tf_op | source)
XLA Modules:
  0.0 456.1 jit_solution(10788636232864134756)
XLA Ops:
  0.6 287.9 %reduce_share.1 = (f32[10368,128]{1,0:T(8,128)}, f32[1,896]{1,0:T(1,128)}, f32[8,128]{1,0:T(8,128)}) custom-call(bf16[16,3,12,1,36864]{4,3,2,1,0:T(2,128)(2,1)} %bitcast.grad, bf16[16,1,896]{2,1,0:T(2,128)(2,1)} %bitcast.15), custom_call_target="tpu_custom_call" | custom-call | tf_op jit(solution)/shard_map/reduce_share/pallas_call | solution.py:279
  288.5 145.7 %update_gather.1 = (bf16[16,3,4,864,128]{4,3,2,1,0:T(8,128)(2,1)S(1)}, f32[3,4,864,128]{3,2,1,0:T(8,128)S(1)}, f32[3,4,864,128]{3,2,1,0:T(8,128)S(1)}, f32[3,4,8...) custom-call(f32[3,4,864,128]{3,2,1,0:T(8,128)} %bitcast.14, ...), custom_call_target="tpu_custom_call" | custom-call | tf_op jit(solution)/shard_map/update_gather/pallas_call | solution.py:458
  434.2 0.0 copy-start.2
  434.2 0.0 copy-start.1
  434.2 0.0 copy-start
  434.2 20.0 %drain.1 = (bf16[16,3,4,864,128]{4,3,2,1,0:T(8,128)(2,1)}, f32[3,4,864,128]{3,2,1,0:T(8,128)}, f32[3,4,864,128]{3,2,1,0:T(8,128)}, f32[3,4,864,128]{3,2,1,0:T(8,128)}, bf16[112,128]{1,0:T(8,128)(2,1)}) custom-call(bf16[16,3,4,864,128]{4,3,2,1,0:T(8,128)(2,1)S(1)} %get-tuple-element.27.refs_0_, f32[3,4,864,128]{3,2,1,0:T(8,128)S(1)} %get-tuple-element.28.refs_1_, ...), custom_call_target="tpu_custom_call" | custom-call | tf_op jit(solution)/shard_map/drain/pallas_call | solution.py:470
  454.3 0.0 copy-done.2
  454.3 0.6 reduce
  454.9 0.0 copy-done.1
  454.9 0.6 reduce.1
  455.5 0.0 copy-done
  455.5 0.6 reduce.2
Async XLA Ops:
  434.2 20.1 %copy-start.2 = (f32[1,896]{1,0:T(1,128)S(1)}, f32[1,896]{1,0:T(1,128)}, u32[]{:S(2)}) copy-start(f32[1,896]{1,0:T(1,128)} %get-tuple-element.35) | copy-start | bytes 10756
  434.2 20.7 %copy-start.1 = (f32[1,896]{1,0:T(1,128)S(1)}, f32[1,896]{1,0:T(1,128)}, u32[]{:S(2)}) copy-start(f32[1,896]{1,0:T(1,128)} %get-tuple-element.36) | copy-start | bytes 10756
  434.2 21.3 %copy-start = (f32[1,896]{1,0:T(1,128)S(1)}, f32[1,896]{1,0:T(1,128)}, u32[]{:S(2)}) copy-start(f32[1,896]{1,0:T(1,128)} %get-tuple-element.37) | copy-start | bytes 10756

commit v4 on v0

v4 whole, which is shorter than its diff:
```python
import functools

import jax
import jax.numpy as jnp
from jax import lax
from jax.experimental import pallas as pl
from jax.experimental.pallas import tpu as pltpu
from jax.sharding import PartitionSpec as P

STEP = 4
LEARN_RATE = 1e-3
BETA_ONE = 0.9
BETA_TWO = 0.999
ADAM_EPS = 1e-8
DECAY = 0.01
NORM_EPS = 1e-6
FIX_ONE = 1.0 - BETA_ONE ** STEP
FIX_TWO = 1.0 - BETA_TWO ** STEP

MESH = pl.DeviceIdType.MESH
LANES = 128
GROUP = 16
STRIDES = (2, 4, 8)
DIMS = tuple(tuple(STRIDES[(c + j) % 3] for j in range(3)) for c in range(3))
PACK_SLOTS = 3
F32 = jnp.float32
BF16 = jnp.bfloat16


def adam_update(grad_sum, clip_coef, master, moment, second, decay):
    clip_grad = clip_coef * grad_sum
    new_moment = BETA_ONE * moment + (1.0 - BETA_ONE) * clip_grad
    new_second = BETA_TWO * second + (1.0 - BETA_TWO) * clip_grad * clip_grad
    step_dir = (new_moment / FIX_ONE) / (jnp.sqrt(new_second / FIX_TWO) + ADAM_EPS)
    new_master = master - LEARN_RATE * (step_dir + decay * master)
    return new_master, new_moment, new_second


def bit_of(index, stride):
    return lax.rem(lax.div(index, stride), 2)


def across(index, stride):
    return index + stride * (1 - 2 * bit_of(index, stride))


def flip(index, strides):
    for stride in strides:
        index = across(index, stride)
    return index


def aligned(start, size):
    return pl.ds(pl.multiple_of(start, 16), size)


def step_kernel(chunks, rows, parts, grad, gvec, master, moment, second, vec_master, vec_moment, vec_second,
                out, state, vec_out, vec_state,
                raw, send_b, keep_b, stage, vec_in, vec_total, vec_share, square, square_in,
                raw_sem, send_a_sem, recv_a_sem, send_b_sem, recv_b_sem, send_c_sem, recv_c_sem,
                vec_send, vec_recv, square_send, square_recv, stage_sem, state_sem,
                send_sem, recv_sem, share_send, share_recv):
    me = lax.axis_index('fsdp')
    core = bit_of(me, 1)
    share_rows = 3 * chunks * rows
    span = share_rows // (3 * parts)

    def packed(c, t, quarter):
        return aligned(((c * PACK_SLOTS + lax.rem(t, PACK_SLOTS)) * 4 + quarter) * 4 * rows, 4 * rows)

    def landed(c, t, j):
        return aligned((3 * PACK_SLOTS * 4 + (c * chunks + t) * 3 + j) * 4 * rows, 4 * rows)

    def half_sums(c, t):
        return aligned(share_rows + (c * chunks + t) * 2 * rows, 2 * rows)

    def totals(c, t):
        return aligned((c * chunks + t) * rows, rows)

    def load(c, t):
        slot = lax.rem(t + c, 2)
        return pltpu.make_async_copy(grad.at[:, c, t], raw.at[slot], raw_sem.at[slot])

    def copy_a(c, t, j):
        d1 = DIMS[c][0]
        mine, other = bit_of(me, d1), across(me, d1)
        device, d1_bit, core_bit = ((across(me, 1), mine, 1 - core), (other, 1 - mine, core),
                                    (across(other, 1), 1 - mine, 1 - core))[j]
        return pltpu.make_async_remote_copy(
            src_ref=out.at[packed(c, t, 2 * d1_bit + core_bit)], dst_ref=out.at[landed(c, t, j)],
            send_sem=send_a_sem.at[c, lax.rem(t, PACK_SLOTS), j], recv_sem=recv_a_sem.at[c, t, j],
            device_id=(device,), device_id_type=MESH)

    def copy_b(c, t):
        s = lax.rem(t, 2)
        return pltpu.make_async_remote_copy(
            src_ref=send_b.at[c, s], dst_ref=state.at[half_sums(c, t)],
            send_sem=send_b_sem.at[c, s], recv_sem=recv_b_sem.at[c, t],
            device_id=(across(me, DIMS[c][1]),), device_id_type=MESH)

    def copy_c(c, t):
        away = 1 - bit_of(me, DIMS[c][2])
        source = aligned(share_rows + ((c * chunks + t) * 2 + away) * rows, rows)
        return pltpu.make_async_remote_copy(
            src_ref=state.at[source], dst_ref=state.at[totals(c, t)],
            send_sem=send_c_sem, recv_sem=recv_c_sem.at[c, t],
            device_id=(across(me, DIMS[c][2]),), device_id_type=MESH)

    blk = 96
    blocks = rows // blk

    def pack(c, t):
        load(c, t).wait()
        slot = lax.rem(t + c, 2)

        @pl.when(t >= PACK_SLOTS)
        def _():
            for j in range(3):
                copy_a(c, t - PACK_SLOTS, j).wait_send()

        base = (c * PACK_SLOTS + lax.rem(t, PACK_SLOTS)) * 16 * rows
        for share in range(GROUP):
            d1_bit, core_bit, d2_bit, d3_bit = [(share // d) % 2 for d in (DIMS[c][0], 1) + DIMS[c][1:]]
            place = 8 * d1_bit + 4 * core_bit + 2 * d2_bit + d3_bit

            def body(b, carry):
                columns = pl.ds(pl.multiple_of(b * blk * LANES, blk * LANES), blk * LANES)
                out[aligned(base + place * rows + b * blk, blk), :] = raw[slot, share, :, columns].reshape(blk, LANES)
                return carry

            lax.fori_loop(0, blocks, body, 0)

    def send_a(c, t):
        for j in range(3):
            copy_a(c, t, j).start()

    def load_after(c, t):
        nc, nt = (c + 2) % 3, t + (c + 2) // 3

        @pl.when(nt < chunks)
        def _():
            load(nc, nt).start()

    def sum_a(c, t):
        d1, d2, d3 = DIMS[c]
        own = ((c * PACK_SLOTS + lax.rem(t, PACK_SLOTS)) * 4 + 2 * bit_of(me, d1) + core) * 4 * rows
        others = [(3 * PACK_SLOTS * 4 + (c * chunks + t) * 3 + j) * 4 * rows for j in range(3)]
        for j in range(3):
            copy_a(c, t, j).wait_recv()

        @pl.when(t >= 2)
        def _():
            copy_b(c, t - 2).wait_send()

        s = lax.rem(t, 2)
        for target, half in ((send_b, 1 - bit_of(me, d2)), (keep_b, bit_of(me, d2))):
            def body(b, carry):
                shift = half * 2 * rows + b * blk
                one, two, three, four = [out[aligned(base + shift, blk), :].astype(F32) for base in [own] + others]
                target[c, s, aligned(b * blk, blk), :] = (one + two) + (three + four)
                return carry

            lax.fori_loop(0, 2 * blocks, body, 0)
            if target is send_b:
                copy_b(c, t).start()

    def sum_b(c, t):
        d3 = DIMS[c][2]
        copy_b(c, t).wait_recv()
        s = lax.rem(t, 2)
        mine = bit_of(me, d3)

        def add(k):
            def body(b, carry):
                held = aligned(share_rows + ((c * chunks + t) * 2 + k) * rows + b * blk, blk)
                state[held, :] = keep_b[c, s, aligned(k * rows + b * blk, blk), :] + state[held, :]
                return carry

            lax.fori_loop(0, blocks, body, 0)

        add(1 - mine)
        copy_c(c, t).start()
        add(mine)

    def sum_c(c, t):
        copy_c(c, t).wait_recv()
        mine = bit_of(me, DIMS[c][2])

        def body(b, running):
            held = aligned(share_rows + ((c * chunks + t) * 2 + mine) * rows + b * blk, blk)
            here = aligned((c * chunks + t) * rows + b * blk, blk)
            total = state[held, :] + state[here, :]
            state[here, :] = total
            return running + jnp.sum((total * total).reshape(blk // 8, 8, LANES), axis=0)

        square[...] += lax.fori_loop(0, blocks, body, jnp.zeros((8, LANES), F32))

    def small_copy(src, dst, k, sends, recvs):
        return pltpu.make_async_remote_copy(
            src_ref=src, dst_ref=dst, send_sem=sends.at[k], recv_sem=recvs.at[k],
            device_id=(lax.rem(me + k, GROUP),), device_id_type=MESH)

    def vec_copy(k):
        return small_copy(gvec.at[lax.rem(me + k, GROUP)], vec_in.at[k], k, vec_send, vec_recv)

    def square_copy(k):
        return small_copy(square, square_in.at[k], k, square_send, square_recv)

    barrier = pltpu.get_barrier_semaphore()
    for k in range(1, GROUP):
        pl.semaphore_signal(barrier, inc=1, device_id=(lax.rem(me + k, GROUP),), device_id_type=MESH)
    for c in range(2):
        load(c, 0).start()
    square[...] = jnp.zeros_like(square)
    pack(0, 0)
    pl.semaphore_wait(barrier, GROUP - 1)
    send_a(0, 0)
    load_after(0, 0)
    for t in range(2):
        for c in range(1 if t == 0 else 0, 3):
            pack(c, t)
            send_a(c, t)
            load_after(c, t)
    for k in range(1, GROUP):
        vec_copy(k).start()

    def tick(u, carry):
        for c in range(3):
            @pl.when(u < chunks)
            def _():
                sum_a(c, u)
        for c in range(3):
            @pl.when((u >= 1) & (u < chunks + 1))
            def _():
                sum_b(c, u - 1)
        for c in range(3):
            @pl.when(u >= 2)
            def _():
                sum_c(c, u - 2)
        for c in range(3):
            @pl.when(u + 2 < chunks)
            def _():
                pack(c, u + 2)
                send_a(c, u + 2)
                load_after(c, u + 2)

        @pl.when(u == chunks // 2)
        def _():
            total = gvec[me].astype(F32)
            for k in range(1, GROUP):
                vec_copy(k).wait()
                total = total + vec_in[k].astype(F32)
            padding = jnp.zeros((1, vec_total.shape[1] - total.shape[1]), F32)
            vec_total[...] = jnp.concatenate([total, padding], axis=1)
            square[0:1, :] += sum((total * total)[:, LANES * k:LANES * (k + 1)] for k in range(total.shape[1] // LANES))

        return carry

    lax.fori_loop(0, chunks + 2, tick, 0)

    for c in range(3):
        for t in range(chunks - PACK_SLOTS, chunks):
            for j in range(3):
                copy_a(c, t, j).wait_send()
    for k in range(1, GROUP):
        square_copy(k).start()

    pltpu.make_async_copy(state.at[pl.ds(0, share_rows)], state.at[pl.ds(0, share_rows)], send_c_sem).wait()
    for c in range(3):
        for t in range(chunks - 2, chunks):
            copy_b(c, t).wait_send()

    order = [(c, k) for k in range(parts) for c in range(3)]

    def place(c, k, which=0):
        return pl.ds(which * share_rows + (c * parts + k) * span, span)

    def master_load(n):
        return pltpu.make_async_copy(master.at[place(*order[n])], stage.at[n % 2], stage_sem.at[n % 2])

    def state_loads(c, k):
        return [pltpu.make_async_copy(src.at[place(c, k)], state.at[place(c, k, 1 + j)], state_sem.at[c, k, j])
                for j, src in enumerate((moment, second))]

    for n, (c, k) in enumerate(order):
        if n < 2:
            master_load(n).start()
        for one in state_loads(c, k):
            one.start()

    whole = square[...]
    for k in range(1, GROUP):
        square_copy(k).wait_recv()
        whole = whole + square_in[k]
    norm = jnp.sqrt(jnp.sum(whole, keepdims=True))
    clip_one = jnp.minimum(1.0, 1.0 / (norm + NORM_EPS))
    clip_coef = jnp.broadcast_to(clip_one, (1, LANES))

    def block(source, c, k):
        return aligned(source * share_rows + (c * parts + k) * span, span)

    def message(c, k, origin, step):
        here = block(flip(me, origin), c, k)
        return pltpu.make_async_remote_copy(
            src_ref=out.at[here], dst_ref=out.at[here],
            send_sem=send_sem, recv_sem=recv_sem.at[c, k, sum(origin) + step],
            device_id=(across(me, step),), device_id_type=MESH)

    def arrived(c, k, origin):
        pltpu.make_async_remote_copy(
            src_ref=out.at[block(me, c, k)], dst_ref=out.at[block(flip(me, origin), c, k)],
            send_sem=send_sem, recv_sem=recv_sem.at[c, k, sum(origin)],
            device_id=(across(me, 1),), device_id_type=MESH).wait_recv()

    def forward(c, k, origin, steps):
        arrived(c, k, origin)
        for step in steps:
            message(c, k, origin, step).start()

    step_blk = 48

    def update(n, c, k):
        def body(b, carry):
            first = (c * parts + k) * span + b * step_blk
            here, there, last = [aligned(first + j * share_rows, step_blk) for j in range(3)]
            p, m, v = adam_update(state[here, :], clip_coef, stage[n % 2, aligned(b * step_blk, step_blk), :],
                                  state[there, :], state[last, :], DECAY)
            state[here, :] = p
            state[there, :] = m
            state[last, :] = v
            out[aligned(me * share_rows + first, step_blk), :] = p.astype(BF16)
            return carry

        lax.fori_loop(0, span // step_blk, body, 0)

    for n, (c, k) in enumerate(order):
        master_load(n).wait()
        for one in state_loads(c, k):
            one.wait()
        update(n, c, k)
        if n + 2 < len(order):
            master_load(n + 2).start()
        for step in DIMS[c] + (1,):
            message(c, k, (), step).start()

    def share_copy(k, source):
        return small_copy(vec_share, vec_out.at[source], k, share_send, share_recv)

    width = vec_share.shape[1]
    old = [x[...].reshape(1, width) for x in (vec_master, vec_moment, vec_second)]
    fresh = adam_update(vec_total[...][:, :width], clip_one, *old, 0.0)
    for j in range(3):
        vec_state[j] = fresh[j]
    vec_share[...] = fresh[0].astype(BF16)
    vec_out[me] = fresh[0].astype(BF16)
    for k in range(1, GROUP):
        share_copy(k, me).start()

    for origin, steps in (((0,), (1, 2)), ((1,), (2,)), ((2,), ()), ((0, 1), (2,)), ((0, 2), ()), ((1, 2), ()), ((0, 1, 2), ())):
        for c in range(3):
            for k in range(parts):
                forward(c, k, tuple(DIMS[c][j] for j in origin), tuple(DIMS[c][j] for j in steps) + (1,))
    for mask in range(8):
        for c in range(3):
            for k in range(parts):
                arrived(c, k, tuple(STRIDES[j] for j in range(3) if mask // 2 ** j % 2) + (1,))
    for k in range(1, GROUP):
        square_copy(k).wait_send()
        share_copy(k, lax.rem(me + GROUP - k, GROUP)).wait()
    sent = pl.ds(0, (GROUP - 1) * share_rows)
    pltpu.make_async_copy(out.at[sent], out.at[sent], send_sem).wait()


def drain_kernel(pieces, weights, state, vec, vec_state, weights_out, master, moment, second,
                 vec_out, vec_master, vec_moment, vec_second, sem):
    copies = []
    share_rows = master.shape[0]
    for src, start, dst, count in ((weights, 0, weights_out, 4 * pieces), (state, 0, master, pieces),
                                   (state, share_rows, moment, pieces), (state, 2 * share_rows, second, pieces)):
        size = dst.shape[0] // count
        copies += [pltpu.make_async_copy(src.at[pl.ds(start + k * size, size)], dst.at[pl.ds(k * size, size)],
                                         sem.at[len(copies) + k]) for k in range(count)]
    copies += [pltpu.make_async_copy(vec_state.at[j, 0], dst, sem.at[len(copies) + j])
               for j, dst in enumerate((vec_master, vec_moment, vec_second))]
    for copy in copies:
        copy.start()
    vec_out[...] = jnp.concatenate([vec[k].astype(F32).reshape(-1, LANES) for k in range(vec.shape[0])], axis=0).astype(BF16)
    for copy in copies:
        copy.wait()


def full_step(grad_mat, grad_vec, state, vec_state, chunks, parts):
    share_rows = grad_mat.shape[1] // GROUP // LANES
    rows = share_rows // (3 * chunks)
    span = share_rows // (3 * parts)
    width = grad_vec.shape[1] // GROUP
    vmem, anywhere = pl.BlockSpec(memory_space=pltpu.VMEM), pl.BlockSpec(memory_space=pl.ANY)
    dma = pltpu.SemaphoreType.DMA
    held = pl.pallas_call(
        functools.partial(step_kernel, chunks, rows, parts),
        out_shape=(pltpu.VMEM((GROUP * share_rows, LANES), BF16), pltpu.VMEM((3 * share_rows, LANES), F32),
                   pltpu.VMEM((GROUP, 1, width), BF16), pltpu.VMEM((3, 1, width), F32)),
        in_specs=[anywhere, vmem] + [anywhere] * 3 + [vmem] * 3,
        out_specs=(vmem,) * 4,
        scratch_shapes=[
            pltpu.VMEM((2, GROUP, 1, rows * LANES), BF16),
            pltpu.VMEM((3, 2, 2 * rows, LANES), F32),
            pltpu.VMEM((3, 2, 2 * rows, LANES), F32),
            pltpu.VMEM((2, span, LANES), F32),
            pltpu.VMEM((GROUP, 1, width), BF16),
            pltpu.VMEM((1, -(-width // 1024) * 1024), F32),
            pltpu.VMEM((1, width), BF16),
            pltpu.VMEM((8, LANES), F32),
            pltpu.VMEM((GROUP, 8, LANES), F32),
            dma((2,)), dma((3, PACK_SLOTS, 3)), dma((3, chunks, 3)), dma((3, 2)), dma((3, chunks)), dma, dma((3, chunks)),
            dma((GROUP,)), dma((GROUP,)), dma((GROUP,)), dma((GROUP,)), dma((2,)), dma((3, parts, 2)),
            dma, dma((3, parts, GROUP)), dma((GROUP,)), dma((GROUP,)),
        ],
        compiler_params=pltpu.CompilerParams(collective_id=0, has_side_effects=True, vmem_limit_bytes=14 * 512 * 1024),
        name='full_step',
    )(grad_mat.reshape(GROUP, 3, chunks, 1, rows * LANES), grad_vec.reshape(GROUP, 1, width),
      *[x.reshape(share_rows, LANES) for x in state], *vec_state)
    pieces = 4
    states = jax.ShapeDtypeStruct((share_rows, LANES), F32)
    vectors = jax.ShapeDtypeStruct((width,), F32)
    weights, *rest = pl.pallas_call(
        functools.partial(drain_kernel, pieces),
        out_shape=(jax.ShapeDtypeStruct((GROUP * share_rows, LANES), BF16), states, states, states,
                   jax.ShapeDtypeStruct((GROUP * width // LANES, LANES), BF16), vectors, vectors, vectors),
        in_specs=[vmem] * 4,
        out_specs=(anywhere,) * 4 + (vmem,) + (anywhere,) * 3,
        scratch_shapes=[dma((7 * pieces + 3,))],
        compiler_params=pltpu.CompilerParams(vmem_limit_bytes=7 * 1024 * 1024),
        name='drain',
    )(*[pltpu.with_memory_space_constraint(x, pltpu.VMEM) for x in held])
    flat = [x.reshape(-1) for x in rest]
    return tuple(flat[:3] + flat[4:] + [weights.reshape(-1), flat[3]])


def solution(mesh):
    def local_step(grad_mat, grad_vec, master_mat, moment_mat, second_mat, master_vec, moment_vec, second_vec):
        return full_step(grad_mat, grad_vec, (master_mat, moment_mat, second_mat),
                         (master_vec, moment_vec, second_vec), 18, 4)

    row_spec = P('fsdp', None)
    flat_spec = P('fsdp')
    whole_spec = P()
    return jax.shard_map(local_step, mesh=mesh,
                         in_specs=(row_spec, row_spec) + (flat_spec,) * 6,
                         out_specs=(flat_spec,) * 6 + (whole_spec, whole_spec),
                         check_vma=False)
```

time: 1460 us -> 445 us (0.30)
  waiting for transfers between devices: 652 us -> 0 us
  Pallas kernels: 0 us -> 444 us
  other arithmetic: 369 us -> 0 us
  local copies, waits for them, and re-layouts: 355 us -> 0 us
  blocking collectives: 46.9 us -> 0 us
  between operations: 16.3 us -> 0.64 us
    all_to_all x2 -> x0, waiting for transfers between devices: 506 us -> none  [total_share(): received = lax.all_to_all(rows, 'fsdp', 0, 0, tiled=True)]
    pallas_call x0 -> x2, Pallas kernels: none -> 444 us  [the longest x1 425 us: full_step(): pl.pallas_call(functools.partial(step_kernel, chunks, rows, parts), out_s...]
    unnamed x15 -> x0, local copies, waits for them, and re-layouts: 355 us -> none
    all_to_all x2 -> x0, other arithmetic: 269 us -> none  [total_share(): received = lax.all_to_all(rows, 'fsdp', 0, 0, tiled=True)]
    all_gather x1 -> x0, waiting for transfers between devices: 146 us -> none  [local_step(): lax.all_gather(new_mat[0].astype(jnp.bfloat16), 'fsdp', tiled=True)]
    reduce_sum x4 -> x0, other arithmetic: 84.3 us -> none  [the longest x2 81.8 us: total_share(): return jnp.sum(received, axis=0, dtype=jnp.float32)]
    psum x1 -> x0, blocking collectives: 32.9 us -> none  [local_step(): total_norm = jnp.sqrt(lax.psum(local_square, 'fsdp'))]
    convert_element_type x2 -> x0, other arithmetic: 15.6 us -> none  [the longest x1 15 us: local_step(): new_mat[0].astype(jnp.bfloat16)]
  transfers between devices with their start and end apart: 3 -> 0, of which waited for: 2 -> 0; matrix products, arithmetic and copies ran while one was open for 34% -> 0% of each run, Pallas kernels for 0% -> 0%
where the time goes in v4:
time: 445 us; the launch traced here: 444 us
  Pallas kernels  444 us (100%)
    pallas_call x1, Pallas kernels, full_step(): pl.pallas_call(functools.partial(step_kernel, chunks, rows, parts), out_s...  425 us
    pallas_call x1, Pallas kernels, full_step(): pl.pallas_call(functools.partial(drain_kernel, pieces), out_shape=(jax.Sh...  19.3 us

profile of v4, /device:TPU:0, one launch (start us, length us, event | category | flops | bytes accessed | tf_op | source)
XLA Modules:
  0.0 444.4 jit_solution(17443794980104304280)
XLA Ops:
  0.6 424.5 %full_step.1 = (bf16[165888,128]{1,0:T(8,128)(2,1)S(1)}, f32[31104,128]{1,0:T(8,128)S(1)}, bf16[16,1,896]{2,1,0:T(2,128)(2,1)S(1)}, f32[3,1,896]{2,1,0:T(1,128)S(1)}) custom-call(bf16[16,3,18,1,24576]{4,3,2,1,0:T(2,128)(2,1)} %bitcast.grad, bf16[16,1,896]{2,1,0:T(2,128)(2,1)} %bitcast.13, f32[10368,128]{1,0:T(8,128)} %bitcast.10, f32[10368,128]{1,0:T(8,128)} %bitcast.11, ...), custom_call_target="tpu_custom_call" | custom-call | tf_op jit(solution)/shard_map/full_step/pallas_call | solution.py:399
  425.2 19.3 %drain.1 = (bf16[165888,128]{1,0:T(8,128)(2,1)}, f32[10368,128]{1,0:T(8,128)}, f32[10368,128]{1,0:T(8,128)}, f32[10368,128]{1,0:T(8,128)}, bf16[112,128]{1,0:T(8...) custom-call(bf16[165888,128]{1,0:T(8,128)(2,1)S(1)} %get-tuple-element.20.weights, ...), custom_call_target="tpu_custom_call" | custom-call | tf_op jit(solution)/shard_map/drain/pallas_call | solution.py:426

commit v5 on v4

--- a/solution.py
+++ b/solution.py
@@ -22,7 +22,7 @@
 GROUP = 16
 STRIDES = (2, 4, 8)
 DIMS = tuple(tuple(STRIDES[(c + j) % 3] for j in range(3)) for c in range(3))
-PACK_SLOTS = 3
+PACK_SLOTS = 4
 F32 = jnp.float32
 BF16 = jnp.bfloat16
 
@@ -56,8 +56,8 @@
 
 def step_kernel(chunks, rows, parts, grad, gvec, master, moment, second, vec_master, vec_moment, vec_second,
                 out, state, vec_out, vec_state,
-                raw, send_b, keep_b, stage, vec_in, vec_total, vec_share, square, square_in,
-                raw_sem, send_a_sem, recv_a_sem, send_b_sem, recv_b_sem, send_c_sem, recv_c_sem,
+                raw, send_b, stage, vec_in, lines, vec_total, vec_share, square, square_in,
+                line_sem, raw_sem, send_a_sem, recv_a_sem, send_b_sem, recv_b_sem, send_c_sem, recv_c_sem,
                 vec_send, vec_recv, square_send, square_recv, stage_sem, state_sem,
                 send_sem, recv_sem, share_send, share_recv):
     me = lax.axis_index('fsdp')
@@ -78,8 +78,7 @@
         return aligned((c * chunks + t) * rows, rows)
 
     def load(c, t):
-        slot = lax.rem(t + c, 2)
-        return pltpu.make_async_copy(grad.at[:, c, t], raw.at[slot], raw_sem.at[slot])
+        return pltpu.make_async_copy(grad.at[:, c, t], raw.at[c], raw_sem.at[c])
 
     def copy_a(c, t, j):
         d1 = DIMS[c][0]
@@ -106,12 +105,11 @@
             send_sem=send_c_sem, recv_sem=recv_c_sem.at[c, t],
             device_id=(across(me, DIMS[c][2]),), device_id_type=MESH)
 
-    blk = 96
+    blk = 192
     blocks = rows // blk
 
     def pack(c, t):
         load(c, t).wait()
-        slot = lax.rem(t + c, 2)
 
         @pl.when(t >= PACK_SLOTS)
         def _():
@@ -125,7 +123,7 @@
 
             def body(b, carry):
                 columns = pl.ds(pl.multiple_of(b * blk * LANES, blk * LANES), blk * LANES)
-                out[aligned(base + place * rows + b * blk, blk), :] = raw[slot, share, :, columns].reshape(blk, LANES)
+                out[aligned(base + place * rows + b * blk, blk), :] = raw[c, share, :, columns].reshape(blk, LANES)
                 return carry
 
             lax.fori_loop(0, blocks, body, 0)
@@ -135,16 +133,17 @@
             copy_a(c, t, j).start()
 
     def load_after(c, t):
-        nc, nt = (c + 2) % 3, t + (c + 2) // 3
-
-        @pl.when(nt < chunks)
+        @pl.when(t + 1 < chunks)
         def _():
-            load(nc, nt).start()
+            load(c, t + 1).start()
+
+    def local_sum(c, t, row):
+        own = ((c * PACK_SLOTS + lax.rem(t, PACK_SLOTS)) * 4 + 2 * bit_of(me, DIMS[c][0]) + core) * 4 * rows
+        others = [(3 * PACK_SLOTS * 4 + (c * chunks + t) * 3 + j) * 4 * rows for j in range(3)]
+        one, two, three, four = [out[aligned(base + row, blk), :].astype(F32) for base in [own] + others]
+        return (one + two) + (three + four)
 
     def sum_a(c, t):
-        d1, d2, d3 = DIMS[c]
-        own = ((c * PACK_SLOTS + lax.rem(t, PACK_SLOTS)) * 4 + 2 * bit_of(me, d1) + core) * 4 * rows
-        others = [(3 * PACK_SLOTS * 4 + (c * chunks + t) * 3 + j) * 4 * rows for j in range(3)]
         for j in range(3):
             copy_a(c, t, j).wait_recv()
 
@@ -152,28 +151,23 @@
         def _():
             copy_b(c, t - 2).wait_send()
 
-        s = lax.rem(t, 2)
-        for target, half in ((send_b, 1 - bit_of(me, d2)), (keep_b, bit_of(me, d2))):
-            def body(b, carry):
-                shift = half * 2 * rows + b * blk
-                one, two, three, four = [out[aligned(base + shift, blk), :].astype(F32) for base in [own] + others]
-                target[c, s, aligned(b * blk, blk), :] = (one + two) + (three + four)
-                return carry
-
-            lax.fori_loop(0, 2 * blocks, body, 0)
-            if target is send_b:
-                copy_b(c, t).start()
+        away = 1 - bit_of(me, DIMS[c][1])
+
+        def body(b, carry):
+            send_b[c, lax.rem(t, 2), aligned(b * blk, blk), :] = local_sum(c, t, away * 2 * rows + b * blk)
+            return carry
+
+        lax.fori_loop(0, 2 * blocks, body, 0)
+        copy_b(c, t).start()
 
     def sum_b(c, t):
-        d3 = DIMS[c][2]
         copy_b(c, t).wait_recv()
-        s = lax.rem(t, 2)
-        mine = bit_of(me, d3)
+        near, mine = bit_of(me, DIMS[c][1]), bit_of(me, DIMS[c][2])
 
         def add(k):
             def body(b, carry):
                 held = aligned(share_rows + ((c * chunks + t) * 2 + k) * rows + b * blk, blk)
-                state[held, :] = keep_b[c, s, aligned(k * rows + b * blk, blk), :] + state[held, :]
+                state[held, :] = local_sum(c, t, (near * 2 + k) * rows + b * blk) + state[held, :]
                 return carry
 
             lax.fori_loop(0, blocks, body, 0)
@@ -209,7 +203,7 @@
     barrier = pltpu.get_barrier_semaphore()
     for k in range(1, GROUP):
         pl.semaphore_signal(barrier, inc=1, device_id=(lax.rem(me + k, GROUP),), device_id_type=MESH)
-    for c in range(2):
+    for c in range(3):
         load(c, 0).start()
     square[...] = jnp.zeros_like(square)
     pack(0, 0)
@@ -221,8 +215,14 @@
             pack(c, t)
             send_a(c, t)
             load_after(c, t)
+    own_vec = pltpu.make_async_copy(gvec.at[me], vec_in.at[0], vec_recv.at[0])
+    own_vec.start()
     for k in range(1, GROUP):
         vec_copy(k).start()
+    old_vec = [pltpu.make_async_copy(src, lines.at[j, 0, pl.ds(0, src.shape[0])], line_sem.at[j])
+               for j, src in enumerate((vec_master, vec_moment, vec_second))]
+    for one in old_vec:
+        one.start()
 
     def tick(u, carry):
         for c in range(3):
@@ -246,7 +246,8 @@
 
         @pl.when(u == chunks // 2)
         def _():
-            total = gvec[me].astype(F32)
+            own_vec.wait()
+            total = vec_in[0].astype(F32)
             for k in range(1, GROUP):
                 vec_copy(k).wait()
                 total = total + vec_in[k].astype(F32)
@@ -347,7 +348,9 @@
         return small_copy(vec_share, vec_out.at[source], k, share_send, share_recv)
 
     width = vec_share.shape[1]
-    old = [x[...].reshape(1, width) for x in (vec_master, vec_moment, vec_second)]
+    for one in old_vec:
+        one.wait()
+    old = [lines[j][:, :width] for j in range(3)]
     fresh = adam_update(vec_total[...][:, :width], clip_one, *old, 0.0)
     for j in range(3):
         vec_state[j] = fresh[j]
@@ -372,7 +375,7 @@
 
 
 def drain_kernel(pieces, weights, state, vec, vec_state, weights_out, master, moment, second,
-                 vec_out, vec_master, vec_moment, vec_second, sem):
+                 vec_out, vec_master, vec_moment, vec_second, vec_flat, sem):
     copies = []
     share_rows = master.shape[0]
     for src, start, dst, count in ((weights, 0, weights_out, 4 * pieces), (state, 0, master, pieces),
@@ -384,7 +387,9 @@
                for j, dst in enumerate((vec_master, vec_moment, vec_second))]
     for copy in copies:
         copy.start()
-    vec_out[...] = jnp.concatenate([vec[k].astype(F32).reshape(-1, LANES) for k in range(vec.shape[0])], axis=0).astype(BF16)
+    vec_flat[...] = jnp.concatenate([vec[k].astype(F32).reshape(-1, LANES) for k in range(vec.shape[0])], axis=0).astype(BF16)
+    copies.append(pltpu.make_async_copy(vec_flat, vec_out, sem.at[len(copies)]))
+    copies[-1].start()
     for copy in copies:
         copy.wait()
 
@@ -400,19 +405,19 @@
         functools.partial(step_kernel, chunks, rows, parts),
         out_shape=(pltpu.VMEM((GROUP * share_rows, LANES), BF16), pltpu.VMEM((3 * share_rows, LANES), F32),
                    pltpu.VMEM((GROUP, 1, width), BF16), pltpu.VMEM((3, 1, width), F32)),
-        in_specs=[anywhere, vmem] + [anywhere] * 3 + [vmem] * 3,
+        in_specs=[anywhere] * 8,
         out_specs=(vmem,) * 4,
         scratch_shapes=[
-            pltpu.VMEM((2, GROUP, 1, rows * LANES), BF16),
-            pltpu.VMEM((3, 2, 2 * rows, LANES), F32),
+            pltpu.VMEM((3, GROUP, 1, rows * LANES), BF16),
             pltpu.VMEM((3, 2, 2 * rows, LANES), F32),
             pltpu.VMEM((2, span, LANES), F32),
             pltpu.VMEM((GROUP, 1, width), BF16),
+            pltpu.VMEM((3, 1, -(-width // 1024) * 1024), F32),
             pltpu.VMEM((1, -(-width // 1024) * 1024), F32),
             pltpu.VMEM((1, width), BF16),
             pltpu.VMEM((8, LANES), F32),
             pltpu.VMEM((GROUP, 8, LANES), F32),
-            dma((2,)), dma((3, PACK_SLOTS, 3)), dma((3, chunks, 3)), dma((3, 2)), dma((3, chunks)), dma, dma((3, chunks)),
+            dma((3,)), dma((3,)), dma((3, PACK_SLOTS, 3)), dma((3, chunks, 3)), dma((3, 2)), dma((3, chunks)), dma, dma((3, chunks)),
             dma((GROUP,)), dma((GROUP,)), dma((GROUP,)), dma((GROUP,)), dma((2,)), dma((3, parts, 2)),
             dma, dma((3, parts, GROUP)), dma((GROUP,)), dma((GROUP,)),
         ],
@@ -428,8 +433,8 @@
         out_shape=(jax.ShapeDtypeStruct((GROUP * share_rows, LANES), BF16), states, states, states,
                    jax.ShapeDtypeStruct((GROUP * width // LANES, LANES), BF16), vectors, vectors, vectors),
         in_specs=[vmem] * 4,
-        out_specs=(anywhere,) * 4 + (vmem,) + (anywhere,) * 3,
-        scratch_shapes=[dma((7 * pieces + 3,))],
+        out_specs=(anywhere,) * 8,
+        scratch_shapes=[pltpu.VMEM((GROUP * width // LANES, LANES), BF16), dma((7 * pieces + 4,))],
         compiler_params=pltpu.CompilerParams(vmem_limit_bytes=7 * 1024 * 1024),
         name='drain',
     )(*[pltpu.with_memory_space_constraint(x, pltpu.VMEM) for x in held])

time: 445 us -> 442 us (level)
  no operation moved by 1% of the time
where the time goes in v5:
time: 442 us
  Pallas kernels  441 us (100%)
    pallas_call x1, Pallas kernels, full_step(): pl.pallas_call(functools.partial(step_kernel, chunks, rows, parts), out_s...  423 us
    pallas_call x1, Pallas kernels, full_step(): pl.pallas_call(functools.partial(drain_kernel, pieces), out_shape=(jax.Sh...  18.7 us

profile of v5, /device:TPU:0, one launch (start us, length us, event | category | flops | bytes accessed | tf_op | source)
XLA Modules:
  0.0 442.0 jit_solution(10240157670703813822)
XLA Ops:
  0.6 422.7 %full_step.1 = (bf16[165888,128]{1,0:T(8,128)(2,1)S(1)}, f32[31104,128]{1,0:T(8,128)S(1)}, bf16[16,1,896]{2,1,0:T(2,128)(2,1)S(1)}, f32[3,1,896]{2,1,0:T(1,128)S(1)}) custom-call(bf16[16,3,18,1,24576]{4,3,2,1,0:T(2,128)(2,1)} %bitcast.grad, bf16[16,1,896]{2,1,0:T(2,128)(2,1)} %bitcast.13, f32[10368,128]{1,0:T(8,128)} %bitcast.10, f32[10368,128]{1,0:T(8,128)} %bitcast.11, ...), custom_call_target="tpu_custom_call" | custom-call | tf_op jit(solution)/shard_map/full_step/pallas_call | solution.py:404
  423.4 18.7 %drain.1 = (bf16[165888,128]{1,0:T(8,128)(2,1)}, f32[10368,128]{1,0:T(8,128)}, f32[10368,128]{1,0:T(8,128)}, f32[10368,128]{1,0:T(8,128)}, bf16[112,128]{1,0:T(8...) custom-call(bf16[165888,128]{1,0:T(8,128)(2,1)S(1)} %get-tuple-element.20.weights, ...), custom_call_target="tpu_custom_call" | custom-call | tf_op jit(solution)/shard_map/drain/pallas_call | solution.py:431

commit v6 on v5

--- a/solution.py
+++ b/solution.py
@@ -318,7 +318,7 @@
         for step in steps:
             message(c, k, origin, step).start()
 
-    step_blk = 48
+    step_blk = 96
 
     def update(n, c, k):
         def body(b, carry):
@@ -359,13 +359,16 @@
     for k in range(1, GROUP):
         share_copy(k, me).start()
 
-    for origin, steps in (((0,), (1, 2)), ((1,), (2,)), ((2,), ()), ((0, 1), (2,)), ((0, 2), ()), ((1, 2), ()), ((0, 1, 2), ())):
-        for c in range(3):
-            for k in range(parts):
-                forward(c, k, tuple(DIMS[c][j] for j in origin), tuple(DIMS[c][j] for j in steps) + (1,))
+    onward = {(0,): (1, 2), (1,): (2,), (0, 1): (2,)}
+    for phase in (((0,), (1,), (2,)), ((0, 1), (0, 2), (1, 2)), ((0, 1, 2),)):
+        for k in range(parts):
+            for c in range(3):
+                for origin in phase:
+                    steps = onward.get(origin, ())
+                    forward(c, k, tuple(DIMS[c][j] for j in origin), tuple(DIMS[c][j] for j in steps) + (1,))
     for mask in range(8):
-        for c in range(3):
-            for k in range(parts):
+        for k in range(parts):
+            for c in range(3):
                 arrived(c, k, tuple(STRIDES[j] for j in range(3) if mask // 2 ** j % 2) + (1,))
     for k in range(1, GROUP):
         square_copy(k).wait_send()

time: 442 us -> 440 us (level)
  no operation moved by 1% of the time
where the time goes in v6:
time: 440 us
  Pallas kernels  439 us (100%)
    pallas_call x1, Pallas kernels, full_step(): pl.pallas_call(functools.partial(step_kernel, chunks, rows, parts), out_s...  421 us
    pallas_call x1, Pallas kernels, full_step(): pl.pallas_call(functools.partial(drain_kernel, pieces), out_shape=(jax.Sh...  18.7 us

profile of v6, /device:TPU:0, one launch (start us, length us, event | category | flops | bytes accessed | tf_op | source)
XLA Modules:
  0.0 439.9 jit_solution(154233960168822921)
XLA Ops:
  0.6 420.6 %full_step.1 = (bf16[165888,128]{1,0:T(8,128)(2,1)S(1)}, f32[31104,128]{1,0:T(8,128)S(1)}, bf16[16,1,896]{2,1,0:T(2,128)(2,1)S(1)}, f32[3,1,896]{2,1,0:T(1,128)S(1)}) custom-call(bf16[16,3,18,1,24576]{4,3,2,1,0:T(2,128)(2,1)} %bitcast.grad, bf16[16,1,896]{2,1,0:T(2,128)(2,1)} %bitcast.13, f32[10368,128]{1,0:T(8,128)} %bitcast.10, f32[10368,128]{1,0:T(8,128)} %bitcast.11, ...), custom_call_target="tpu_custom_call" | custom-call | tf_op jit(solution)/shard_map/full_step/pallas_call | solution.py:407
  421.3 18.7 %drain.1 = (bf16[165888,128]{1,0:T(8,128)(2,1)}, f32[10368,128]{1,0:T(8,128)}, f32[10368,128]{1,0:T(8,128)}, f32[10368,128]{1,0:T(8,128)}, bf16[112,128]{1,0:T(8...) custom-call(bf16[165888,128]{1,0:T(8,128)(2,1)S(1)} %get-tuple-element.20.weights, ...), custom_call_target="tpu_custom_call" | custom-call | tf_op jit(solution)/shard_map/drain/pallas_call | solution.py:434

commit v7 on v6

--- a/solution.py
+++ b/solution.py
@@ -128,6 +128,21 @@
 
             lax.fori_loop(0, blocks, body, 0)
 
+    def pack_quarter(c, j):
+        d1, d2, d3 = DIMS[c]
+        mine = bit_of(me, d1)
+        d1_bit, core_bit = ((mine, 1 - core), (1 - mine, core), (1 - mine, 1 - core), (mine, core))[j]
+        for part in range(4):
+            share = d1_bit * d1 + core_bit + part // 2 * d2 + part % 2 * d3
+            first = ((c * PACK_SLOTS * 4 + 2 * d1_bit + core_bit) * 4 + part) * rows
+
+            def body(b, carry):
+                columns = pl.ds(pl.multiple_of(b * blk * LANES, blk * LANES), blk * LANES)
+                out[aligned(first + b * blk, blk), :] = raw[c, share, :, columns].reshape(blk, LANES)
+                return carry
+
+            lax.fori_loop(0, blocks, body, 0)
+
     def send_a(c, t):
         for j in range(3):
             copy_a(c, t, j).start()
@@ -206,15 +221,23 @@
     for c in range(3):
         load(c, 0).start()
     square[...] = jnp.zeros_like(square)
-    pack(0, 0)
+    for c in range(3):
+        load(c, 0).wait()
+        pack_quarter(c, 1)
     pl.semaphore_wait(barrier, GROUP - 1)
-    send_a(0, 0)
-    load_after(0, 0)
-    for t in range(2):
-        for c in range(1 if t == 0 else 0, 3):
-            pack(c, t)
-            send_a(c, t)
-            load_after(c, t)
+    for c in range(3):
+        copy_a(c, 0, 1).start()
+    for j in (2, 0):
+        for c in range(3):
+            pack_quarter(c, j)
+            copy_a(c, 0, j).start()
+    for c in range(3):
+        pack_quarter(c, 3)
+        load_after(c, 0)
+    for c in range(3):
+        pack(c, 1)
+        send_a(c, 1)
+        load_after(c, 1)
     own_vec = pltpu.make_async_copy(gvec.at[me], vec_in.at[0], vec_recv.at[0])
     own_vec.start()
     for k in range(1, GROUP):

time: 440 us -> 440 us (level)
  no operation moved by 1% of the time
where the time goes in v7:
time: 440 us
  Pallas kernels  439 us (100%)
    pallas_call x1, Pallas kernels, full_step(): pl.pallas_call(functools.partial(step_kernel, chunks, rows, parts), out_s...  421 us
    pallas_call x1, Pallas kernels, full_step(): pl.pallas_call(functools.partial(drain_kernel, pieces), out_shape=(jax.Sh...  18.7 us

profile of v7, /device:TPU:0, one launch (start us, length us, event | category | flops | bytes accessed | tf_op | source)
XLA Modules:
  0.0 439.9 jit_solution(12899279563689788370)
XLA Ops:
  0.6 420.6 %full_step.1 = (bf16[165888,128]{1,0:T(8,128)(2,1)S(1)}, f32[31104,128]{1,0:T(8,128)S(1)}, bf16[16,1,896]{2,1,0:T(2,128)(2,1)S(1)}, f32[3,1,896]{2,1,0:T(1,128)S(1)}) custom-call(bf16[16,3,18,1,24576]{4,3,2,1,0:T(2,128)(2,1)} %bitcast.grad, bf16[16,1,896]{2,1,0:T(2,128)(2,1)} %bitcast.13, f32[10368,128]{1,0:T(8,128)} %bitcast.10, f32[10368,128]{1,0:T(8,128)} %bitcast.11, ...), custom_call_target="tpu_custom_call" | custom-call | tf_op jit(solution)/shard_map/full_step/pallas_call | solution.py:430
  421.3 18.7 %drain.1 = (bf16[165888,128]{1,0:T(8,128)(2,1)}, f32[10368,128]{1,0:T(8,128)}, f32[10368,128]{1,0:T(8,128)}, f32[10368,128]{1,0:T(8,128)}, bf16[112,128]{1,0:T(8...) custom-call(bf16[165888,128]{1,0:T(8,128)(2,1)S(1)} %get-tuple-element.20.weights, ...), custom_call_target="tpu_custom_call" | custom-call | tf_op jit(solution)/shard_map/drain/pallas_call | solution.py:457
